TPU v7x, 256 devices: a whole 4x4x8 slice. The times are simulated.
256 devices in a mesh: dp: 256 (over z, y, x, core).
Axes of the slice: x: 4, y: 4, z: 8, core: 2. Of those that a mesh axis runs over, the one named last changes fastest.
Arguments:
- query_feat: bfloat16 [32768, 256], P('dp')
- item_feat: bfloat16 [32768, 256], P('dp')
- log_q: float32 [32768], P('dp')
- w_query_in: bfloat16 [256, 256], replicated
- w_query_out: bfloat16 [256, 128], replicated
- w_item_in: bfloat16 [256, 256], replicated
- w_item_out: bfloat16 [256, 128], replicated
Outputs:
- output 1: float32 [1], replicated
- output 2: float32 [256, 256], replicated
- output 3: float32 [256, 128], replicated
- output 4: float32 [256, 256], replicated
- output 5: float32 [256, 128], replicated
All inputs are finite; a program needn't handle non-finite values.
Results may differ from a plain program's by a relative error of at most 0.00618852.
Values are sent between devices in bfloat16 or wider.
A program may use at most 768 MiB of HBM per device.

v0:
```python
import jax
import jax.numpy as jnp
from jax import lax
from jax.sharding import PartitionSpec as P

value_a11 = 0.05
NORM_EPS = 1e-6


def tower_forward(feat_rows, w_in, w_out):
    pre_act = jnp.dot(feat_rows, w_in, preferred_element_type=jnp.float32)
    hidden = jnp.maximum(pre_act, 0.0).astype(jnp.bfloat16)
    embed = jnp.dot(hidden, w_out, preferred_element_type=jnp.float32)
    inv_norm = lax.rsqrt(jnp.sum(embed * embed, axis=-1, keepdims=True) + NORM_EPS)
    return pre_act, hidden, inv_norm, embed * inv_norm


def tower_backward(feat_rows, w_out, pre_act, hidden, inv_norm, unit_vec, d_unit):
    d_embed = inv_norm * (d_unit - unit_vec * jnp.sum(unit_vec * d_unit, axis=-1, keepdims=True))
    d_embed_bf = d_embed.astype(jnp.bfloat16)
    grad_out = jnp.einsum('bh,be->he', hidden, d_embed_bf, preferred_element_type=jnp.float32)
    d_hidden = jnp.einsum('be,he->bh', d_embed_bf, w_out, preferred_element_type=jnp.float32)
    d_pre = jnp.where(pre_act > 0, d_hidden, 0.0).astype(jnp.bfloat16)
    grad_in = jnp.einsum('bf,bh->fh', feat_rows, d_pre, preferred_element_type=jnp.float32)
    return grad_in, grad_out


def softmax_grads(query_bf, items_all, logq_all, row_offset):
    local_rows, embed_dim = query_bf.shape
    total_rows = items_all.shape[0]
    block_rows = min(local_rows, 256)
    num_blocks = local_rows // block_rows
    grad_scale = 1.0 / (value_a11 * total_rows)
    col_ids = lax.broadcasted_iota(jnp.int32, (1, total_rows), 1)
    row_iota = lax.broadcasted_iota(jnp.int32, (block_rows, 1), 0)
    query_blocks = query_bf.reshape(num_blocks, block_rows, embed_dim)

    def block_step(d_item_acc, inputs):
        block_index, query_blk = inputs
        logits = jnp.einsum('qe,ke->qk', query_blk, items_all, preferred_element_type=jnp.float32) / value_a11 - logq_all[None, :]
        is_pos = (row_offset + block_index * block_rows + row_iota) == col_ids
        row_max = jnp.max(logits, axis=1, keepdims=True)
        log_norm = row_max + jnp.log(jnp.sum(jnp.exp(logits - row_max), axis=1, keepdims=True))
        pos_logit = jnp.sum(jnp.where(is_pos, logits, 0.0), axis=1, keepdims=True)
        prob_rows = jnp.exp(logits - log_norm)
        grad_logits = jnp.where(is_pos, prob_rows - 1.0, prob_rows).astype(jnp.bfloat16)
        d_query_blk = jnp.einsum('qk,ke->qe', grad_logits, items_all, preferred_element_type=jnp.float32) * grad_scale
        d_item_acc = d_item_acc + jnp.einsum('qk,qe->ke', grad_logits, query_blk, preferred_element_type=jnp.float32)
        return d_item_acc, (jnp.sum(log_norm - pos_logit), d_query_blk)

    acc_init = jnp.zeros((total_rows, embed_dim), jnp.float32)
    d_item_acc, (loss_parts, d_query_blocks) = lax.scan(block_step, acc_init, (jnp.arange(num_blocks), query_blocks))
    return jnp.sum(loss_parts), d_query_blocks.reshape(local_rows, embed_dim), d_item_acc * grad_scale


def solution(mesh):
    group = mesh.shape['dp']

    def local_step(query_feat, item_feat, log_q, w_query_in, w_query_out, w_item_in, w_item_out):
        local_rows = query_feat.shape[0]
        total_rows = local_rows * group
        q_pre, q_hidden, q_inv, q_unit = tower_forward(query_feat, w_query_in, w_query_out)
        v_pre, v_hidden, v_inv, v_unit = tower_forward(item_feat, w_item_in, w_item_out)
        items_all = lax.all_gather(v_unit.astype(jnp.bfloat16), 'dp', axis=0, tiled=True)
        logq_all = lax.all_gather(log_q, 'dp', axis=0, tiled=True)
        row_offset = lax.axis_index('dp') * local_rows
        loss_sum, d_query, d_item_part = softmax_grads(q_unit.astype(jnp.bfloat16), items_all, logq_all, row_offset)
        d_item = lax.psum_scatter(d_item_part, 'dp', scatter_dimension=0, tiled=True)
        grad_query_in, grad_query_out = tower_backward(query_feat, w_query_out, q_pre, q_hidden, q_inv, q_unit, d_query)
        grad_item_in, grad_item_out = tower_backward(item_feat, w_item_out, v_pre, v_hidden, v_inv, v_unit, d_item)
        loss = jnp.reshape(lax.psum(loss_sum, 'dp') / total_rows, (1,))
        return (loss, lax.psum(grad_query_in, 'dp'), lax.psum(grad_query_out, 'dp'), lax.psum(grad_item_in, 'dp'), lax.psum(grad_item_out, 'dp'))

    return jax.shard_map(local_step, mesh=mesh, in_specs=(P('dp', None), P('dp', None), P('dp'), P(), P(), P(), P()), out_specs=(P(), P(), P(), P(), P()), check_vma=False)
```

profile of v0, /device:TPU:1, one launch (start us, length us, event | category | flops | bytes accessed | tf_op | source)
XLA Modules:
  0.0 1748.5 jit_solution(4865341555841295329)
XLA Ops:
  7.2 0.0 copy-start
  7.2 0.0 all-gather.3.cloned.1.call-start
  7.2 0.9 copy-done
  8.1 1.0 fusion.20
  9.1 1.1 multiply_reduce_fusion.2
  10.2 0.6 multiply_convert_fusion.2
  10.8 0.0 all-gather.3.cloned.1.call-update
  10.8 0.0 reduce-scatter.2.cloned.1.call-start
  10.9 79.2 %all-gather = f32[256,1,128]{2,1,0:T(1,128)S(1)} all-gather(f32[1,1,128]{2,1,0:T(1,128)} %bitcast.26), channel_id=1, replica_groups=mesh['dp'=256] {'dp'}, dimensions={0}, use_global_device_ids=true | all-gather | bytes 131584 | tf_op jit(solution)/shard_map/all_gather | solution.py:65
  90.1 1.1 fusion.19
  91.2 1.1 multiply_reduce_fusion.3
  92.2 42.4 %all-gather.3.cloned.1.call-done = bf16[32768,128]{0,1:T(8,128)(2,1)} async-done(((bf16[128,128]{0,1:T(8,128)(2,1)}), bf16[32768,128]{0,1:T(8,128)(2,1)}) %all-gather.3.cloned.1.call-update) | async-done | bytes 8388624 | tf_op jit(solution)/shard_map/all_gather | solution.py:64
  134.6 5.0 fusion.18
  139.7 5.0 select_reduce_fusion
  144.7 0.6 subtract_reduce_fusion
  145.3 4.0 fusion.1
  149.3 0.0 copy-start.1
  149.3 3.2 copy-done.1
  152.5 8.1 convolution_multiply_fusion
  160.5 0.0 reduce-scatter.2.cloned.1.call-update
  160.6 0.0 copy-start.2
  160.6 0.0 copy-start.4
  160.6 0.0 copy-start.3
  160.6 0.0 copy-start.5
  160.6 0.0 all-reduce.3.cloned.1.call-start
  160.7 8.1 multiply_reduce_fusion.1
  168.8 0.9 fusion.8
  169.7 0.0 copy-done.2
  169.7 0.0 copy-done.4
  169.7 1.1 convolution_bitcast_fusion.1
  170.8 1292.7 %reduce-scatter.2.cloned.1.call-done = f32[128,128]{0,1:T(8,128)} async-done(((f32[32768,128]{0,1:T(8,128)}), f32[128,128]{0,1:T(8,128)}) %reduce-scatter.2.cloned.1.call-update) | async-done | bytes 65552 | tf_op jit(solution)/shard_map/reduce_scatter | solution.py:68
  1463.5 0.9 multiply_reduce_fusion
  1464.4 0.9 multiply_convert_fusion
  1465.2 0.9 fusion.10
  1466.1 0.0 copy-done.3
  1466.1 0.0 copy-done.5
  1466.1 1.1 convolution_bitcast_fusion
  1467.2 0.0 all-reduce.3.cloned.1.call-update
  1467.2 80.1 %psum.35 = f32[]{:T(128)} all-reduce(f32[]{:T(128)} %get-tuple-element.51), channel_id=1, replica_groups=mesh['dp'=256] {'dp'}, use_global_device_ids=true, to_apply=%region_6.7 | all-reduce | flops 1 | bytes 8 | tf_op jit(solution)/shard_map/psum | solution.py:71
  1548.0 186.2 %all-reduce.3.cloned.1.call-done = (f32[256,256]{0,1:T(8,128)}, f32[256,128]{1,0:T(8,128)}, f32[256,256]{0,1:T(8,128)}, f32[256,128]{1,0:T(8,128)}) async-done(((f32[256,256]{0,1:T(8,128)}, f32[256,128]{1,0:T(8,128)}, f32[256,256]{0,1:T(8,128)}, f32[256,128]{1,0:T(8,128)}), (f32[256,256]{0,1:T(8,128)}, f32[256,128]{1,0:T(8,128)}, f32[256,256]{0,1:T(8,128)}, ...) | async-done | bytes 786448 | tf_op jit(solution)/shard_map/psum | solution.py:72
  1734.1 1.8 copy.16
  1735.9 1.8 copy.17
  1737.7 1.6 copy.23
  1739.3 1.6 copy.24
  (4 shorter events, 0.0 us)
Async XLA Ops:
  7.2 0.9 copy-start
  7.2 127.4 %all-gather.3.cloned.1.call-start = ((), (), s32[]{:S(2)}) async-start(), calls=%async_computation.1 | async-start | bytes 8421376 | tf_op jit(solution)/shard_map/all_gather | solution.py:64
  10.8 1452.7 %reduce-scatter.2.cloned.1.call-start = ((), (), s32[]{:S(2)}) async-start(), calls=%async_computation.2 | async-start | bytes 16842752 | tf_op jit(solution)/shard_map/reduce_scatter | solution.py:68
  149.3 3.2 copy-start.1
  160.6 9.1 copy-start.2
  160.6 9.1 copy-start.4
  160.6 1305.5 %copy-start.3 = (bf16[128,256]{1,0:T(8,128)(2,1)S(1)}, bf16[128,256]{1,0:T(8,128)(2,1)}, u32[]{:S(2)}) copy-start(bf16[128,256]{1,0:T(8,128)(2,1)} %param.8) | copy-start | bytes 196612
  160.6 1305.5 %copy-start.5 = (bf16[256,128]{1,0:T(8,128)(2,1)S(1)}, bf16[256,128]{1,0:T(8,128)(2,1)}, u32[]{:S(2)}) copy-start(bf16[256,128]{1,0:T(8,128)(2,1)} %param.13) | copy-start | bytes 196612
  160.6 1573.5 %all-reduce.3.cloned.1.call-start = ((), (), s32[]{:S(2)}) async-start(), calls=%async_computation.3 | async-start | bytes 1572864 | tf_op jit(solution)/shard_map/psum | solution.py:72
Sparse Core Ops, SparseCore 0:
  12.3 122.2 all-gather.2
  160.7 1302.7 reduce-scatter.1
  1470.0 264.1 all-reduce.2
where the time goes:
time: 1750 us
  waiting for transfers between devices  1520 us (87%)
  blocking collectives  159 us (9%)
  matrix products  29.4 us (2%)
    reduce_scatter x1, waiting for transfers between devices, local_step(): lax.psum_scatter(d_item_part, 'dp', scatter_dimension=0, tiled=True)  1290 us
    psum x1, waiting for transfers between devices, local_step(): lax.psum(grad_query_in, 'dp')  186 us
    psum x1, blocking collectives, local_step(): loss = jnp.reshape(lax.psum(loss_sum, 'dp') / total_rows, (1,))  80.1 us
    all_gather x1, blocking collectives, local_step(): logq_all = lax.all_gather(log_q, 'dp', axis=0, tiled=True)  79.2 us
    all_gather x1, waiting for transfers between devices, local_step(): lax.all_gather(v_unit.astype(jnp.bfloat16), 'dp', axis=0, tiled=True)  42.4 us
  transfers between devices with their start and end apart: 3, of which 3 were waited for; matrix products, arithmetic and copies ran while one was open for 1% of the time, Pallas kernels for 0%

commit v1 on v0

v1 whole, which is shorter than its diff:
```python
import functools

import jax
import jax.numpy as jnp
from jax import lax
from jax.experimental import pallas as pl
from jax.experimental.pallas import tpu as pltpu
from jax.sharding import PartitionSpec as P

f32, bf16 = jnp.float32, jnp.bfloat16
MESH = pl.DeviceIdType.MESH
TEMP = 0.05
EPS = 1e-6
LOG2E = 1.4426950408889634
LN2 = 0.6931471805599453
NT = (((1,), (1,)), ((), ()))
TN = (((0,), (0,)), ((), ()))
NN = (((1,), (0,)), ((), ()))


def dot(a, b, dims=NN):
    return lax.dot_general(a, b, dims, preferred_element_type=f32)


def kernel(NZ, NXY, qf, vf, lq, wqi, wqo, wvi, wvo,
           gqi_o, gqo_o, gvi_o, gvo_o, loss_o,
           u_all, v_all, vt, lq_all, bcol, e_all, g_all, csum, stats, invl,
           up, ui, uh, ua, vp, vi, vh, va,
           su, ru, pv_out, pv_in, sv, rv, gl, gpair, gx_s, gx_r, gz_r, fin, loss_p, loss_x,
           s_u, r_u, s_v, r_v, s_lq, r_lq, s_st, r_st, s_pv, r_pv, s_sv, r_sv, s_su, r_su,
           s_gp, r_gp, s_gx, r_gx, s_gz, r_gz, s_ag, r_ag, s_rl, r_rl, s_lp, r_lp, s_lx, r_lx, s_vr):
    R, D = 128, 128
    NQ = NZ * R
    NI = 2 * NXY * R
    B = NZ * NXY * 2 * R
    CH = 768 // NXY
    me = lax.axis_index("dp")
    c = lax.rem(me, 2)
    j = lax.rem(lax.div(me, 2), NXY)
    z = lax.div(me, 2 * NXY)

    def dev(zz, jj, cc):
        return ((zz * NXY + jj) * 2 + cc,)

    zpeers = [lax.rem(z + k, NZ) for k in range(1, NZ)]
    xpeers = [lax.rem(j + k, NXY) for k in range(1, NXY)]
    oc = 1 - c
    slot = c * NXY + j

    def send(src, dst, ss, rs, to):
        pltpu.make_async_remote_copy(src_ref=src, dst_ref=dst, send_sem=ss, recv_sem=rs,
                                     device_id=to, device_id_type=MESH).start()

    def wait(ref, sem):
        pltpu.make_async_copy(ref, ref, sem).wait()

    bar = pltpu.get_barrier_semaphore()
    npeer = 0
    for zz in zpeers:
        pl.semaphore_signal(bar, inc=1, device_id=dev(zz, j, c), device_id_type=MESH); npeer += 1
    for jj in xpeers:
        for cc in (c, oc):
            pl.semaphore_signal(bar, inc=1, device_id=dev(z, jj, cc), device_id_type=MESH); npeer += 1
    pl.semaphore_signal(bar, inc=1, device_id=dev(z, j, oc), device_id_type=MESH); npeer += 1

    def tower(x, wi, wo, unit, inv, hid, act):
        a = dot(x[...], wi[...])
        h = jnp.maximum(a, 0.0).astype(bf16)
        e = dot(h, wo[...])
        r = lax.rsqrt(jnp.sum(e * e, axis=-1, keepdims=True) + EPS)
        u = e * r
        unit[...] = u
        inv[...] = jnp.broadcast_to(r, (R, 128))
        hid[...] = h
        act[...] = a
        return u.astype(bf16)

    u_bf = tower(qf, wqi, wqo, up, ui, uh, ua)
    v_bf = tower(vf, wvi, wvo, vp, vi, vh, va)
    u_all[pl.ds(z * R, R), :] = u_bf
    v_all[pl.ds(slot * R, R), :] = v_bf
    lq_all[slot] = lq[...]
    pos = jnp.sum(u_bf.astype(f32) * v_bf.astype(f32), axis=0, keepdims=True) * (1.0 / TEMP) - lq[...]
    stats[z, :, pl.ds(NQ + 128, 128)] = pos

    pl.semaphore_wait(bar, npeer)
    mine_v = v_all.at[pl.ds(slot * R, R), :]
    mine_u = u_all.at[pl.ds(z * R, R), :]
    for jj in xpeers:
        for cc in (c, oc):
            send(lq_all.at[slot], lq_all.at[slot], s_lq, r_lq, dev(z, jj, cc))
    send(lq_all.at[slot], lq_all.at[slot], s_lq, r_lq, dev(z, j, oc))
    for zz in zpeers:
        send(mine_u, mine_u, s_u, r_u.at[z], dev(zz, j, c))
    for jj in xpeers:
        send(mine_v, mine_v, s_v, r_v.at[slot], dev(z, jj, c))
    send(mine_v, mine_v, s_vr, r_v.at[slot], dev(z, j, oc))

    wait(lq_all.at[pl.ds(0, 2 * NXY - 1)], r_lq)
    m2 = jnp.max(-lq_all[...], axis=(0, 1, 2), keepdims=True)[0] * LOG2E
    m2 = jnp.broadcast_to(m2, (1, 128))
    stats[z, :, pl.ds(NQ, 128)] = m2

    def bias(k, _):
        row = lq_all[k] * LOG2E + m2
        bcol[pl.ds(k * R, R), :] = jnp.transpose(jnp.broadcast_to(row, (128, 128)))
        return 0
    lax.fori_loop(0, 2 * NXY, bias, 0)

    for k, jj in enumerate(xpeers):
        sl = c * NXY + jj
        ref = v_all.at[pl.ds(sl * R, R), :]
        wait(ref, r_v.at[sl])
        send(ref, ref, s_vr, r_v.at[sl], dev(z, j, oc))
    for zz in zpeers:
        wait(u_all.at[pl.ds(zz * R, R), :], r_u.at[zz])
    for jj in range(NXY):
        sl = oc * NXY + jj
        wait(v_all.at[pl.ds(sl * R, R), :], r_v.at[sl])

    csum[...] = jnp.zeros_like(csum)
    QC = min(256, NQ)

    def pass1(g, _):
        rows = pl.ds(g * 256, 256)
        vb = v_all[rows, :]
        bc = bcol[rows, :]
        for qc in range(NQ // QC):
            cols = slice(qc * QC, (qc + 1) * QC)
            s = dot(vb, u_all[cols, :], NT)
            e = jnp.exp2(s * (LOG2E / TEMP) - jnp.concatenate([bc] * (QC // 128), axis=1))
            e_all[rows, cols] = e
            csum[:, cols] += jnp.sum(e.reshape(32, 8, QC), axis=0)
        vt[:, rows] = jnp.transpose(vb.astype(f32)).astype(bf16)
        return 0
    lax.fori_loop(0, NI // 256, pass1, 0)

    stats[z, :, pl.ds(0, NQ)] = jnp.sum(csum[...], axis=0, keepdims=True)
    for zz in zpeers:
        send(stats.at[z], stats.at[z], s_st, r_st, dev(zz, j, c))
    wait(stats.at[pl.ds(0, NZ - 1)], r_st)
    ms = [stats[k, :, NQ:NQ + 128] for k in range(NZ)]
    mx = functools.reduce(jnp.maximum, ms)
    tot = jnp.zeros((1, NQ), f32)
    for k in range(NZ):
        w = jnp.exp2(ms[k] - mx)
        tot = tot + stats[k, :, 0:NQ] * jnp.concatenate([w] * NZ, axis=1)
    mine_w = jnp.exp2(m2 - mx)
    invl[...] = jnp.concatenate([mine_w] * NZ, axis=1) / tot
    lse = (jnp.log2(tot) + jnp.concatenate([mx] * NZ, axis=1)) * LN2
    lrow = jnp.zeros((1, 128), f32)
    for k in range(NZ):
        lrow = lrow + (lse[:, k * 128:(k + 1) * 128] - stats[k, :, NQ + 128:NQ + 256])
    loss_p[c] = lrow
    send(loss_p.at[c], loss_p.at[c], s_lp, r_lp, dev(z, j, oc))

    def g_block(g):
        rows = pl.ds(g * 256, 256)
        il = invl[...]
        g_all[rows, :] = (e_all[rows, :] * il).astype(bf16)

        @pl.when(lax.div(slot, 2) == g)
        def _():
            rr = pl.ds(slot * R, R)
            qq = pl.ds(pl.multiple_of(z * R, 128), R)
            eye = lax.broadcasted_iota(jnp.int32, (R, R), 0) == lax.broadcasted_iota(jnp.int32, (R, R), 1)
            p = e_all[rr, qq] * invl[:, qq]
            g_all[rr, qq] = jnp.where(eye, p - 1.0, p).astype(bf16)
        return dot(g_all[rows, :], u_all[...])

    def first_half(k, _):
        g = oc * (NXY // 2) + k
        d = g_block(g)
        for t in range(2):
            jj = 2 * k + t
            pv_out[jj] = d[t * 128:(t + 1) * 128, :]
            send(pv_out.at[jj], pv_in.at[jj], s_pv, r_pv.at[jj], dev(z, j, oc))
        return 0
    lax.fori_loop(0, NXY // 2, first_half, 0)

    def second_half(k, _):
        g = c * (NXY // 2) + k
        d = g_block(g)
        for t in range(2):
            jj = 2 * k + t
            wait(pv_in.at[jj], r_pv.at[jj])
            sv[jj] = d[t * 128:(t + 1) * 128, :] + pv_in[jj]

            @pl.when(jj != j)
            def _():
                send(sv.at[jj], rv.at[j], s_sv, r_sv, dev(z, jj, c))
        return 0
    lax.fori_loop(0, NXY // 2, second_half, 0)
    rv[j] = sv[j]

    def du_part(n, _):
        cols = pl.ds(pl.multiple_of(n * QC, 128), QC)
        d = dot(vt[...], g_all[:, cols])
        for t in range(QC // 128):
            zz = n * (QC // 128) + t
            su[zz] = d[:, t * 128:(t + 1) * 128]

            @pl.when(zz != z)
            def _():
                send(su.at[zz], ru.at[z], s_su, r_su, dev(zz, j, c))
        return 0
    lax.fori_loop(0, NQ // QC, du_part, 0)
    ru[z] = su[z]

    wait(loss_p.at[oc], r_lp)
    loss_x[j] = loss_p[0] + loss_p[1]
    for jj in xpeers:
        send(loss_x.at[j], loss_x.at[j], s_lx, r_lx, dev(z, jj, c))

    def backward(du, x, wo, unit, inv, hid, act, t):
        u, r = unit[...], inv[...]
        de = (r * (du - u * jnp.sum(u * du, axis=-1, keepdims=True))).astype(bf16)
        go = dot(hid[...], de, TN)
        dh = dot(de, wo[...], NT)
        da = jnp.where(act[...] > 0, dh, 0.0).astype(bf16)
        gi = dot(x[...], da, TN)
        gl[t, 0:256, :] = gi[:, 0:128]
        gl[t, 256:512, :] = gi[:, 128:256]
        gl[t, 512:768, :] = go

    scale = 1.0 / (TEMP * B)
    wait(ru.at[pl.ds(0, NZ - 1)], r_su)
    acc = ru[0]
    for k in range(1, NZ):
        acc = acc + ru[k]
    backward(jnp.transpose(acc) * scale, qf, wqo, up, ui, uh, ua, 0)

    wait(rv.at[pl.ds(0, NXY - 1)], r_sv)
    acc = rv[0]
    for k in range(1, NXY):
        acc = acc + rv[k]
    backward(acc * scale, vf, wvo, vp, vi, vh, va, 1)

    send(gl.at[oc], gpair, s_gp, r_gp, dev(z, j, oc))
    wait(gpair, r_gp)
    gx_s[...] = (gl[c] + gpair[...]).reshape(NXY, CH, 128)
    for jj in xpeers:
        send(gx_s.at[jj], gx_r.at[j], s_gx, r_gx, dev(z, jj, c))
    gx_r[j] = gx_s[j]
    wait(gx_r.at[pl.ds(0, NXY - 1)], r_gx)
    acc = gx_r[0]
    for k in range(1, NXY):
        acc = acc + gx_r[k]
    gz_r[z] = acc
    for zz in zpeers:
        send(gz_r.at[z], gz_r.at[z], s_gz, r_gz, dev(zz, j, c))
    wait(gz_r.at[pl.ds(0, NZ - 1)], r_gz)
    acc = gz_r[0]
    for k in range(1, NZ):
        acc = acc + gz_r[k]
    fin[c, j] = acc
    for jj in xpeers:
        send(fin.at[c, j], fin.at[c, j], s_ag, r_ag.at[j], dev(z, jj, c))
    send(fin.at[c, j], fin.at[c, j], s_rl, r_rl.at[j], dev(z, j, oc))
    for jj in xpeers:
        wait(fin.at[c, jj], r_ag.at[jj])
        send(fin.at[c, jj], fin.at[c, jj], s_rl, r_rl.at[jj], dev(z, j, oc))
    wait(loss_x.at[pl.ds(0, NXY - 1)], r_lx)
    ls = loss_x[0]
    for k in range(1, NXY):
        ls = ls + loss_x[k]
    loss_o[...] = jnp.broadcast_to(jnp.sum(ls, axis=-1, keepdims=True) * (1.0 / B), (1, 128))
    for jj in range(NXY):
        wait(fin.at[oc, jj], r_rl.at[jj])
    for t, (gi, go) in enumerate(((gqi_o, gqo_o), (gvi_o, gvo_o))):
        full = fin[t].reshape(768, 128)
        gi[:, 0:128] = full[0:256]
        gi[:, 128:256] = full[256:512]
        go[...] = full[512:768]

    for k in range(2 * NXY - 1):
        pass
    wait(lq_all.at[pl.ds(0, 2 * NXY - 1)], s_lq)
    wait(u_all.at[pl.ds(0, (NZ - 1) * R), :], s_u)
    wait(v_all.at[pl.ds(0, (NXY - 1) * R), :], s_v)
    wait(v_all.at[pl.ds(0, NXY * R), :], s_vr)
    wait(stats.at[pl.ds(0, NZ - 1)], s_st)
    wait(loss_p.at[0], s_lp)
    wait(pv_out, s_pv)
    wait(sv.at[pl.ds(0, NXY - 1)], s_sv)
    wait(su.at[pl.ds(0, NZ - 1)], s_su)
    wait(loss_x.at[pl.ds(0, NXY - 1)], s_lx)
    wait(gpair, s_gp)
    wait(gx_s.at[pl.ds(0, NXY - 1)], s_gx)
    wait(gz_r.at[pl.ds(0, NZ - 1)], s_gz)
    wait(gx_s.at[pl.ds(0, NXY - 1)], s_ag)
    wait(gx_s, s_rl)


def build(NZ, NXY):
    def step(query_feat, item_feat, log_q, w_query_in, w_query_out, w_item_in, w_item_out):
        R = 128
        NQ, NI, CH = NZ * R, 2 * NXY * R, 768 // NXY
        V = pltpu.VMEM
        vm = pl.BlockSpec(memory_space=pltpu.VMEM)
        S = pltpu.SemaphoreType.DMA
        out = pl.pallas_call(
            functools.partial(kernel, NZ, NXY),
            name="two_tower",
            out_shape=[jax.ShapeDtypeStruct((256, 256), f32), jax.ShapeDtypeStruct((256, 128), f32),
                       jax.ShapeDtypeStruct((256, 256), f32), jax.ShapeDtypeStruct((256, 128), f32),
                       jax.ShapeDtypeStruct((1, 128), f32)],
            in_specs=[vm] * 7,
            out_specs=[vm] * 5,
            scratch_shapes=[
                V((NQ, 128), bf16), V((NI, 128), bf16), V((128, NI), bf16), V((2 * NXY, 1, 128), f32),
                V((NI, 128), f32), V((NI, NQ), f32), V((NI, NQ), bf16), V((8, NQ), f32),
                V((NZ, 1, NQ + 256), f32), V((1, NQ), f32),
                V((R, 128), f32), V((R, 128), f32), V((R, 256), bf16), V((R, 256), f32),
                V((R, 128), f32), V((R, 128), f32), V((R, 256), bf16), V((R, 256), f32),
                V((NZ, 128, 128), f32), V((NZ, 128, 128), f32),
                V((NXY, 128, 128), f32), V((NXY, 128, 128), f32), V((NXY, 128, 128), f32), V((NXY, 128, 128), f32),
                V((2, 768, 128), f32), V((768, 128), f32), V((NXY, CH, 128), f32), V((NXY, CH, 128), f32),
                V((NZ, CH, 128), f32), V((2, NXY, CH, 128), f32), V((2, 1, 128), f32), V((NXY, 1, 128), f32),
                S, S((NZ,)), S, S((2 * NXY,)), S, S, S, S, S, S((NXY,)), S, S, S, S,
                S, S, S, S, S, S, S, S((NXY,)), S, S((NXY,)), S, S, S, S, S,
            ],
            compiler_params=pltpu.CompilerParams(collective_id=0, has_side_effects=True, vmem_limit_bytes=60 * 2**20),
        )(query_feat, item_feat, log_q.reshape(1, 128), w_query_in, w_query_out, w_item_in, w_item_out)
        gqi, gqo, gvi, gvo, loss = out
        return loss[0, 0:1], gqi, gqo, gvi, gvo
    return step


def solution(mesh):
    n = mesh.shape["dp"]
    NZ, NXY = (8, 16) if n == 256 else (2, 4)
    return jax.shard_map(build(NZ, NXY), mesh=mesh,
                         in_specs=(P("dp", None), P("dp", None), P("dp"), P(), P(), P(), P()),
                         out_specs=(P(), P(), P(), P(), P()), check_vma=False)
```

time: 1750 us -> 90.5 us (0.05)
  waiting for transfers between devices: 1520 us -> 0 us
  blocking collectives: 159 us -> 0 us
  Pallas kernels: 0 us -> 83.8 us
  matrix products: 29.4 us -> 0 us
    reduce_scatter x1 -> x0, waiting for transfers between devices: 1290 us -> none  [local_step(): lax.psum_scatter(d_item_part, 'dp', scatter_dimension=0, tiled=True)]
    psum x1 -> x0, waiting for transfers between devices: 186 us -> none  [local_step(): lax.psum(grad_query_in, 'dp')]
    pallas_call x0 -> x1, Pallas kernels: none -> 83.8 us  [step(): pl.pallas_call(functools.partial(kernel, NZ, NXY), name='two_tower', out_...]
    psum x1 -> x0, blocking collectives: 80.1 us -> none  [local_step(): loss = jnp.reshape(lax.psum(loss_sum, 'dp') / total_rows, (1,))]
    all_gather x1 -> x0, blocking collectives: 79.2 us -> none  [local_step(): logq_all = lax.all_gather(log_q, 'dp', axis=0, tiled=True)]
    all_gather x1 -> x0, waiting for transfers between devices: 42.4 us -> none  [local_step(): lax.all_gather(v_unit.astype(jnp.bfloat16), 'dp', axis=0, tiled=True)]
    dot_general x11 -> x0, matrix products: 29.4 us -> none  [the longest x1 8.14 us: block_step(): jnp.einsum('qk,ke->qe', grad_logits, items_all, preferred_element_type=jn...]
  transfers between devices with their start and end apart: 3 -> 0, of which waited for: 3 -> 0; matrix products, arithmetic and copies ran while one was open for 1% -> 0% of each run, Pallas kernels for 0% -> 0%
where the time goes in v1:
time: 90.5 us; the launch traced here: 90.3 us
  Pallas kernels  83.8 us (93%)
  local copies, waits for them, and re-layouts  4.69 us (5%)
  between operations  1.84 us (2%)
    pallas_call x1, Pallas kernels, step(): pl.pallas_call(functools.partial(kernel, NZ, NXY), name='two_tower', out_...  83.8 us
    unnamed x12, local copies, waits for them, and re-layouts  4.69 us

profile of v1, /device:TPU:1, one launch (start us, length us, event | category | flops | bytes accessed | tf_op | source)
XLA Modules:
  0.0 90.3 jit_solution(16635196433863548836)
XLA Ops:
  0.6 83.8 %two_tower.1 = (f32[256,256]{1,0:T(8,128)}, f32[256,128]{1,0:T(8,128)}, f32[256,256]{1,0:T(8,128)}, f32[256,128]{1,0:T(8,128)}, f32[1,128]{1,0:T(1,128)}) custom-call(bf16[128,256]{1,0:T(8,128)(2,1)} %qf.1, bf16[128,256]{1,0:T(8,128)(2,1)} %vf.1, f32[1,128]{1,0:T(1,128)} %bitcast.3, bf16[256,256]{1,0:T(8,128)(2,1)} %wqi.1, bf16[256,128]{1,0:T(8,128)(2,1)} %wqo.1, ...), custom_call_target="tpu_custom_call" | custom-call | tf_op jit(solution)/shard_map/two_tower/pallas_call | solution.py:302
  84.4 0.0 copy-start.3
  84.4 0.6 copy-done.3
  85.1 0.0 copy-start.2
  85.1 0.0 copy-start
  85.2 1.7 %copy.18 = f32[256,256]{1,0:T(8,128)} copy(f32[256,256]{1,0:T(8,128)} %get-tuple-element.21) | data formatting | bytes 524288
  86.9 0.0 copy-done.2
  86.9 0.7 copy.19
  87.5 0.0 copy-done
  87.5 0.0 copy-start.1
  87.5 0.7 copy.20
  88.2 0.3 copy-done.1
  88.5 0.7 copy.21
Async XLA Ops:
  84.4 0.7 copy-start.3
  85.1 1.7 %copy-start.2 = (f32[256,128]{1,0:T(8,128)S(1)}, f32[256,128]{1,0:T(8,128)}, u32[]{:S(2)}) copy-start(f32[256,128]{1,0:T(8,128)} %get-tuple-element.22) | copy-start | bytes 393220
  85.1 2.4 %copy-start = (f32[256,256]{1,0:T(8,128)S(1)}, f32[256,256]{1,0:T(8,128)}, u32[]{:S(2)}) copy-start(f32[256,256]{1,0:T(8,128)} %get-tuple-element.23) | copy-start | bytes 786436
  87.5 1.0 %copy-start.1 = (f32[256,128]{1,0:T(8,128)S(1)}, f32[256,128]{1,0:T(8,128)}, u32[]{:S(2)}) copy-start(f32[256,128]{1,0:T(8,128)} %get-tuple-element.24) | copy-start | bytes 393220

commit v2 on v0

v2 whole, which is shorter than its diff:
```python
import functools

import jax
import jax.numpy as jnp
from jax import lax
from jax.experimental import pallas as pl
from jax.experimental.pallas import tpu as pltpu
from jax.sharding import PartitionSpec as P

f32, bf16 = jnp.float32, jnp.bfloat16
MESH = pl.DeviceIdType.MESH
TEMP = 0.05
EPS = 1e-6
LOG2E = 1.4426950408889634
LN2 = 0.6931471805599453
NT = (((1,), (1,)), ((), ()))
TN = (((0,), (0,)), ((), ()))
NN = (((1,), (0,)), ((), ()))
R = 128
GR = 256


class Scope:
    def __init__(self):
        self.cur = None

    def __call__(self, name):
        if self.cur is not None:
            self.cur.__exit__(None, None, None)
        self.cur = None
        if name:
            self.cur = jax.named_scope(name)
            self.cur.__enter__()


def dot(a, b, dims=NN):
    return lax.dot_general(a, b, dims, preferred_element_type=f32)


def ring(n):
    return sorted(range(n), key=lambda k: (min(k, n - k), k))


def torus(ny, nx):
    def dist(o):
        return min(o[0], ny - o[0]) + min(o[1], nx - o[1])
    return sorted(((a, b) for a in range(ny) for b in range(nx)), key=lambda o: (dist(o), o))


def kernel(NZ, NY, NX, qf_h, vf_h, lq_h, wqi_h, wqo_h, wvi_h, wvo_h, fin, loss_o,
           qf, vf, lq, wqi, wqo, wvi, wvo, s_in,
           u_all, v_all, vt, lq_all, bcol, e_all, g_all, csum, stats, invl, invt,
           up, ui, uh, ua, vp, vi, vh, va,
           su, ru, pv_out, pv_in, sv, rv, gl, gpair, gx_s, gx_r, gz_r, loss_p, loss_x,
           s_u, r_u, s_v, r_v, s_lq, r_lq, s_st, r_st, s_pv, r_pv, s_sv, r_sv, s_su, r_su,
           s_gp, r_gp, s_gx, r_gx, s_gz, r_gz, s_ag, r_ag, s_rl, r_rl, s_lp, r_lp, s_lx, r_lx, s_vr):
    sc = Scope()
    NXY = NY * NX
    NQ = NZ * R
    NI = 2 * NXY * R
    B = NZ * NI
    CH = 384 // NXY
    LV = NZ // 2
    SL = NXY // LV
    QC = 2 * R
    IR = 2 * SL * R
    NG = IR // GR
    zoff, xoff = ring(NZ), torus(NY, NX)
    me = lax.axis_index("dp")
    c = lax.rem(me, 2)
    j = lax.rem(lax.div(me, 2), NXY)
    y, x = lax.div(j, NX), lax.rem(j, NX)
    z = lax.div(me, 2 * NXY)
    oc = 1 - c

    def dev(zz, jj, cc):
        return ((zz * NXY + jj) * 2 + cc,)

    def zs(k, sign):
        o = zoff[k]
        return lax.rem(z + (o if sign > 0 else NZ - o), NZ)

    def xs(k, sign):
        a, b = xoff[k]
        yy = lax.rem(y + (a if sign > 0 else NY - a), NY)
        xx = lax.rem(x + (b if sign > 0 else NX - b), NX)
        return yy * NX + xx

    def slot(k, core):
        return (k // SL) * 2 * SL + core * SL + k % SL

    def send(src, dst, ss, rs, to):
        pltpu.make_async_remote_copy(src_ref=src, dst_ref=dst, send_sem=ss, recv_sem=rs,
                                     device_id=to, device_id_type=MESH).start()

    def wait(ref, sem):
        pltpu.make_async_copy(ref, ref, sem).wait()

    def vrows(s):
        return v_all.at[pl.ds(s * R, R), :]

    sc("barsig")
    bar = pltpu.get_barrier_semaphore()
    peers = [dev(zs(k, 1), j, c) for k in range(1, NZ)]
    peers += [dev(z, xs(k, 1), cc) for k in range(1, NXY) for cc in (c, oc)]
    peers += [dev(z, j, oc)]
    for p in peers:
        pl.semaphore_signal(bar, inc=1, device_id=p, device_id_type=MESH)
    loads = [pltpu.make_async_copy(a, b, s_in.at[i]) for i, (a, b) in enumerate(
        ((qf_h, qf), (wqi_h, wqi), (wqo_h, wqo), (vf_h, vf), (wvi_h, wvi), (wvo_h, wvo), (lq_h, lq)))]
    for cp in loads:
        cp.start()
    for cp in loads:
        cp.wait()

    sc("tower")

    def tower(xr, wi, wo, unit, inv, hid, act):
        a = dot(xr[...], wi[...])
        h = jnp.maximum(a, 0.0).astype(bf16)
        e = dot(h, wo[...])
        r = lax.rsqrt(jnp.sum(e * e, axis=-1, keepdims=True) + EPS)
        u = e * r
        unit[...] = u
        inv[...] = jnp.broadcast_to(r, (R, 128))
        hid[...] = h
        act[...] = a
        return u.astype(bf16)

    u_bf = tower(qf, wqi, wqo, up, ui, uh, ua)
    v_bf = tower(vf, wvi, wvo, vp, vi, vh, va)
    u_all[0:R, :] = u_bf
    v_all[0:R, :] = v_bf
    lq_all[0] = lq[...]
    pos = jnp.sum(u_bf.astype(f32) * v_bf.astype(f32), axis=0, keepdims=True) * (1.0 / TEMP) - lq[...]
    stats[z, :, pl.ds(NQ + 128, 128)] = pos
    csum[...] = jnp.zeros_like(csum)

    sc("barwait")
    pl.semaphore_wait(bar, len(peers))
    sc("sends")
    mine_u, mine_v = u_all.at[pl.ds(0, R), :], vrows(0)
    for k in range(1, NXY):
        for core, cc in ((0, c), (1, oc)):
            send(lq_all.at[0], lq_all.at[slot(k, core)], s_lq, r_lq, dev(z, xs(k, 1), cc))
    send(lq_all.at[0], lq_all.at[slot(0, 1)], s_lq, r_lq, dev(z, j, oc))
    send(mine_v, vrows(slot(0, 1)), s_vr, r_v.at[slot(0, 1)], dev(z, j, oc))
    for k in range(1, NXY):
        if k < NZ:
            send(mine_u, u_all.at[pl.ds(k * R, R), :], s_u, r_u.at[k], dev(zs(k, 1), j, c))
        send(mine_v, vrows(slot(k, 0)), s_v, r_v.at[slot(k, 0)], dev(z, xs(k, 1), c))

    sc("lqwait")
    wait(lq_all.at[pl.ds(0, 2 * NXY - 1)], r_lq)
    sc("bias")
    nl = -lq_all[...].reshape(2 * NXY, 128)
    m2 = jnp.max(jnp.max(nl, axis=0, keepdims=True), axis=1, keepdims=True) * LOG2E
    m2 = jnp.broadcast_to(m2, (1, 128))
    stats[z, :, pl.ds(NQ, 128)] = m2
    bt = jnp.transpose(m2 - nl * LOG2E)
    for s in range(2 * NXY):
        bcol[s * R:(s + 1) * R, :] = jnp.broadcast_to(bt[:, s:s + 1], (R, 128))

    def block(rows, cols):
        s = dot(v_all[rows, :], u_all[cols, :], NT)
        b = bcol[rows, :]
        e = jnp.exp2(s * (LOG2E / TEMP) - jnp.concatenate([b, b], axis=1))
        e_all[rows, cols] = e
        csum[:, cols] += jnp.sum(e.reshape(GR // 8, 8, QC), axis=0)

    def grp(g):
        return pl.ds(pl.multiple_of(g * GR, GR), GR)

    def qcols(l):
        return slice(l * QC, (l + 1) * QC)

    def new_items(l, g):
        for l2 in range(l + 1):
            block(grp(g), qcols(l2))
        vt[:, grp(g)] = jnp.transpose(v_all[grp(g), :].astype(f32)).astype(bf16)

    def loop(lo, n, f):
        lax.fori_loop(0, n, lambda i, u: (f(lo + i), u)[1], 0)

    for l in range(LV):
        sc(f"uwait{l}")
        for k in (2 * l, 2 * l + 1):
            if k:
                wait(u_all.at[pl.ds(k * R, R), :], r_u.at[k])
        sc(f"vwait{l}")
        for k in range(l * SL, (l + 1) * SL):
            if k:
                s = slot(k, 0)
                wait(vrows(s), r_v.at[s])
                send(vrows(s), vrows(slot(k, 1)), s_vr, r_v.at[slot(k, 1)], dev(z, j, oc))
        sc(f"pass1_{l}a")
        if l:
            loop(0, l * NG, lambda g: block(grp(g), qcols(l)))
        sc(f"pass1_{l}b")
        loop(l * NG, NG // 2, functools.partial(new_items, l))
        sc(f"vwait{l}p")
        for k in range(l * SL, (l + 1) * SL):
            s = slot(k, 1)
            wait(vrows(s), r_v.at[s])
        sc(f"pass1_{l}c")
        loop(l * NG + NG // 2, NG // 2, functools.partial(new_items, l))

    sc("stats_send")
    tot = jnp.sum(csum[...], axis=0, keepdims=True)
    for k in range(NZ):
        stats[z, :, pl.ds(pl.multiple_of(zs(k, -1) * R, R), R)] = tot[:, k * R:(k + 1) * R]
    for k in range(1, NZ):
        send(stats.at[z], stats.at[z], s_st, r_st, dev(zs(k, 1), j, c))
    sc("stats_wait")
    wait(stats.at[pl.ds(0, NZ - 1)], r_st)
    sc("stats_comp")
    ms = [stats[k, :, NQ:NQ + 128] for k in range(NZ)]
    mx = functools.reduce(jnp.maximum, ms)
    tot = jnp.zeros((1, NQ), f32)
    for k in range(NZ):
        tot = tot + stats[k, :, 0:NQ] * jnp.concatenate([jnp.exp2(ms[k] - mx)] * NZ, axis=1)
    invt[...] = jnp.concatenate([jnp.exp2(m2 - mx)] * NZ, axis=1) / tot
    for k in range(NZ):
        invl[:, k * R:(k + 1) * R] = invt[:, pl.ds(pl.multiple_of(zs(k, -1) * R, R), R)]
    lse = (jnp.log2(tot) + jnp.concatenate([mx] * NZ, axis=1)) * LN2
    lrow = jnp.zeros((1, 128), f32)
    for k in range(NZ):
        lrow = lrow + (lse[:, k * R:(k + 1) * R] - stats[k, :, NQ + 128:NQ + 256])
    loss_p[c] = lrow
    send(loss_p.at[c], loss_p.at[c], s_lp, r_lp, dev(z, j, oc))

    def norm(rows, c0, c1):
        cols = slice(c0 * QC, c1 * QC)
        g_all[rows, cols] = (e_all[rows, cols] * invl[:, cols]).astype(bf16)

    def dv(g):
        return dot(g_all[g * GR:(g + 1) * GR, :], u_all[...])

    pend = []

    def flush():
        for k in pend:
            wait(pv_in.at[k], r_pv.at[k])
            sv[k] = sv[k] + pv_in[k]
            if k:
                send(sv.at[k], rv.at[k], s_sv, r_sv, dev(z, xs(k, -1), c))
        pend.clear()

    def dv_level(l, c0, c1):
        sc(f"dv{l}")
        for t in range(SL // 2):
            for core in (1, 0):
                g = l * NG + core * (NG // 2) + t
                if c1 > c0:
                    norm(slice(g * GR, (g + 1) * GR), c0, c1)
                d = dv(g)
                ks = (l * SL + 2 * t, l * SL + 2 * t + 1)
                for i, k in enumerate(ks):
                    if core:
                        pv_out[k] = d[i * R:(i + 1) * R, :]
                        send(pv_out.at[k], pv_in.at[k], s_pv, r_pv.at[k], dev(z, j, oc))
                    else:
                        sv[k] = d[i * R:(i + 1) * R, :]
            flush()
            pend.extend(ks)

    def du_level(l, nrows):
        sc(f"du{l}")
        loop(0, nrows // GR, lambda g: norm(grp(g), l, l + 1))
        if l == 0:
            eye = lax.broadcasted_iota(jnp.int32, (R, R), 0) == lax.broadcasted_iota(jnp.int32, (R, R), 1)
            p = e_all[0:R, 0:R] * invl[:, 0:R]
            g_all[0:R, 0:R] = jnp.where(eye, p - 1.0, p).astype(bf16)
        d = dot(vt[...], g_all[:, qcols(l)])
        for i in range(2):
            k = 2 * l + i
            su[k] = d[:, i * R:(i + 1) * R]
            if k:
                send(su.at[k], ru.at[k], s_su, r_su, dev(zs(k, -1), j, c))

    dv_level(LV - 1, 0, LV)
    half = (LV + 1) // 2
    for l in range(LV - 1, half - 1, -1):
        du_level(l, (LV - 1) * IR)
    if LV > 2:
        dv_level(LV - 2, 0, half)
    rest = LV - 2 if LV > 2 else LV - 1
    for l in range(half - 1, -1, -1):
        du_level(l, rest * IR)
    for l in range(rest - 1, -1, -1):
        dv_level(l, 0, 0)
    sc("flush")
    flush()

    sc("loss")
    wait(loss_p.at[oc], r_lp)
    loss_x[j] = loss_p[0] + loss_p[1]
    for k in range(1, NXY):
        send(loss_x.at[j], loss_x.at[j], s_lx, r_lx, dev(z, xs(k, 1), c))

    def backward(du, xr, wo, unit, inv, hid, act, t):
        u, r = unit[...], inv[...]
        de = (r * (du - u * jnp.sum(u * du, axis=-1, keepdims=True))).astype(bf16)
        go = dot(hid[...], de, TN)
        dh = dot(de, wo[...], NT)
        da = jnp.where(act[...] > 0, dh, 0.0).astype(bf16)
        gi = dot(xr[...], da, TN)
        gl[t, 0:256, :] = gi[:, 0:128]
        gl[t, 256:512, :] = gi[:, 128:256]
        gl[t, 512:768, :] = go
        send(gl.at[t, pl.ds(pl.multiple_of(oc * 384, 8), 384), :], gpair.at[t], s_gp.at[t], r_gp.at[t], dev(z, j, oc))

    def pair_sum(t):
        sc(f"gp_wait{t}")
        wait(gpair.at[t], r_gp.at[t])
        gx_s[t] = (gl[t, pl.ds(pl.multiple_of(c * 384, 8), 384), :] + gpair[t]).reshape(NXY, CH, 128)
        for k in range(1, NXY):
            to = xs(k, 1)
            send(gx_s.at[t, to], gx_r.at[t, j], s_gx.at[t], r_gx.at[t], dev(z, to, c))
        gx_r[t, j] = gx_s[t, j]

    def plane_sum(t):
        sc(f"gx_wait{t}")
        wait(gx_r.at[t, pl.ds(0, NXY - 1)], r_gx.at[t])
        acc = gx_r[t, 0]
        for k in range(1, NXY):
            acc = acc + gx_r[t, k]
        gz_r[t, z] = acc
        for k in range(1, NZ):
            send(gz_r.at[t, z], gz_r.at[t, z], s_gz.at[t], r_gz.at[t], dev(zs(k, 1), j, c))

    def ring_sum(t):
        sc(f"gz_wait{t}")
        wait(gz_r.at[t, pl.ds(0, NZ - 1)], r_gz.at[t])
        acc = gz_r[t, 0]
        for k in range(1, NZ):
            acc = acc + gz_r[t, k]
        fin[t, c, j] = acc
        for k in range(1, NXY):
            send(fin.at[t, c, j], fin.at[t, c, j], s_ag.at[t], r_ag.at[t, k], dev(z, xs(k, 1), c))
        send(fin.at[t, c, j], fin.at[t, c, j], s_rl.at[t], r_rl.at[t, 0], dev(z, j, oc))

    def relay(t):
        sc(f"ag_wait{t}")
        for k in range(1, NXY):
            ref = fin.at[t, c, xs(k, -1)]
            wait(ref, r_ag.at[t, k])
            send(ref, ref, s_rl.at[t], r_rl.at[t, k], dev(z, j, oc))

    scale = 1.0 / (TEMP * B)
    sc("ru_wait")
    wait(ru.at[pl.ds(0, NZ - 1)], r_su)
    sc("bwd_q")
    acc = su[0]
    for k in range(1, NZ):
        acc = acc + ru[k]
    backward(jnp.transpose(acc) * scale, qf, wqo, up, ui, uh, ua, 0)
    pair_sum(0)
    sc("rv_wait")
    wait(rv.at[pl.ds(0, NXY - 1)], r_sv)
    sc("bwd_v")
    acc = sv[0]
    for k in range(1, NXY):
        acc = acc + rv[k]
    backward(acc * scale, vf, wvo, vp, vi, vh, va, 1)
    pair_sum(1)
    plane_sum(0)
    plane_sum(1)
    ring_sum(0)
    ring_sum(1)
    relay(0)
    relay(1)
    sc("loss2")
    wait(loss_x.at[pl.ds(0, NXY - 1)], r_lx)
    ls = loss_x[0]
    for k in range(1, NXY):
        ls = ls + loss_x[k]
    loss_o[...] = jnp.broadcast_to(jnp.sum(ls, axis=-1, keepdims=True) * (1.0 / B), (1, 128))
    sc("rl_wait")
    for t in range(2):
        for k in range(NXY):
            wait(fin.at[t, oc, xs(k, -1)], r_rl.at[t, k])

    sc("sendwait")
    wait(lq_all.at[pl.ds(0, 2 * NXY - 1)], s_lq)
    wait(u_all.at[pl.ds(0, (NZ - 1) * R), :], s_u)
    wait(v_all.at[pl.ds(0, (NXY - 1) * R), :], s_v)
    wait(v_all.at[pl.ds(0, NXY * R), :], s_vr)
    wait(stats.at[pl.ds(0, NZ - 1)], s_st)
    wait(loss_p.at[0], s_lp)
    wait(pv_out, s_pv)
    wait(sv.at[pl.ds(0, NXY - 1)], s_sv)
    wait(su.at[pl.ds(0, NZ - 1)], s_su)
    wait(loss_x.at[pl.ds(0, NXY - 1)], s_lx)
    for t in range(2):
        wait(gpair.at[t], s_gp.at[t])
        wait(gx_s.at[t, pl.ds(0, NXY - 1)], s_gx.at[t])
        wait(gz_r.at[t, pl.ds(0, NZ - 1)], s_gz.at[t])
        wait(gx_s.at[t, pl.ds(0, NXY - 1)], s_ag.at[t])
        wait(gx_s.at[t], s_rl.at[t])
    sc(None)


def emit(fin, loss, gqi, gqo, gvi, gvo, loss_o):
    for t, (gi, go) in enumerate(((gqi, gqo), (gvi, gvo))):
        gi[:, 0:128] = fin[t, 0:256]
        gi[:, 128:256] = fin[t, 256:512]
        go[...] = fin[t, 512:768]
    loss_o[...] = loss[...]


def build(NZ, NY, NX):
    def step(query_feat, item_feat, log_q, w_query_in, w_query_out, w_item_in, w_item_out):
        NXY = NY * NX
        NQ, NI, CH = NZ * R, 2 * NXY * R, 384 // NXY
        V, S = pltpu.VMEM, pltpu.SemaphoreType.DMA
        vm, hbm = pl.BlockSpec(memory_space=pltpu.VMEM), pl.BlockSpec(memory_space=pl.ANY)
        sd = jax.ShapeDtypeStruct
        tower = [V((R, 128), f32), V((R, 128), f32), V((R, 256), bf16), V((R, 256), f32)]
        fin, loss = pl.pallas_call(
            functools.partial(kernel, NZ, NY, NX),
            name="two_tower",
            out_shape=[sd((2, 2, NXY, CH, 128), f32), sd((1, 128), f32)],
            in_specs=[hbm] * 7,
            out_specs=[vm] * 2,
            scratch_shapes=[
                V((R, 256), bf16), V((R, 256), bf16), V((1, 128), f32),
                V((256, 256), bf16), V((256, 128), bf16), V((256, 256), bf16), V((256, 128), bf16), S((7,)),
                V((NQ, 128), bf16), V((NI, 128), bf16), V((128, NI), bf16), V((2 * NXY, 1, 128), f32),
                V((NI, 128), f32), V((NI, NQ), f32), V((NI, NQ), bf16), V((8, NQ), f32),
                V((NZ, 1, NQ + 256), f32), V((1, NQ), f32), V((1, NQ), f32),
                *tower, *tower,
                V((NZ, 128, 128), f32), V((NZ, 128, 128), f32),
                V((NXY, 128, 128), f32), V((NXY, 128, 128), f32), V((NXY, 128, 128), f32), V((NXY, 128, 128), f32),
                V((2, 768, 128), f32), V((2, 384, 128), f32), V((2, NXY, CH, 128), f32), V((2, NXY, CH, 128), f32),
                V((2, NZ, CH, 128), f32), V((2, 1, 128), f32), V((NXY, 1, 128), f32),
                S, S((NZ,)), S, S((2 * NXY,)), S, S, S, S, S, S((NXY,)), S, S, S, S,
                S((2,)), S((2,)), S((2,)), S((2,)), S((2,)), S((2,)), S((2,)), S((2, NXY)), S((2,)), S((2, NXY)),
                S, S, S, S, S,
            ],
            compiler_params=pltpu.CompilerParams(collective_id=0, has_side_effects=True, vmem_limit_bytes=60 * 2**20),
        )(query_feat, item_feat, log_q.reshape(1, 128), w_query_in, w_query_out, w_item_in, w_item_out)
        gqi, gqo, gvi, gvo, out = pl.pallas_call(
            emit,
            name="emit",
            out_shape=[sd((256, 256), f32), sd((256, 128), f32), sd((256, 256), f32), sd((256, 128), f32), sd((1, 128), f32)],
            in_specs=[vm] * 2,
            out_specs=[vm] * 5,
        )(fin.reshape(2, 768, 128), loss)
        return out[0, 0:1], gqi, gqo, gvi, gvo
    return step


def solution(mesh):
    n = mesh.shape["dp"]
    dims = (8, 4, 4) if n == 256 else (4, 2, 2)
    return jax.shard_map(build(*dims), mesh=mesh,
                         in_specs=(P("dp", None), P("dp", None), P("dp"), P(), P(), P(), P()),
                         out_specs=(P(), P(), P(), P(), P()), check_vma=False)
```

time: 1750 us -> 75.4 us (0.04)
  waiting for transfers between devices: 1520 us -> 0 us
  blocking collectives: 159 us -> 0 us
  Pallas kernels: 0 us -> 74.6 us
  matrix products: 29.4 us -> 0 us
    reduce_scatter x1 -> x0, waiting for transfers between devices: 1290 us -> none  [local_step(): lax.psum_scatter(d_item_part, 'dp', scatter_dimension=0, tiled=True)]
    psum x1 -> x0, waiting for transfers between devices: 186 us -> none  [local_step(): lax.psum(grad_query_in, 'dp')]
    psum x1 -> x0, blocking collectives: 80.1 us -> none  [local_step(): loss = jnp.reshape(lax.psum(loss_sum, 'dp') / total_rows, (1,))]
    all_gather x1 -> x0, blocking collectives: 79.2 us -> none  [local_step(): logq_all = lax.all_gather(log_q, 'dp', axis=0, tiled=True)]
    pallas_call x0 -> x2, Pallas kernels: none -> 74.6 us  [the longest x1 72.6 us: step(): pl.pallas_call(functools.partial(kernel, NZ, NY, NX), name='two_tower', o...]
    all_gather x1 -> x0, waiting for transfers between devices: 42.4 us -> none  [local_step(): lax.all_gather(v_unit.astype(jnp.bfloat16), 'dp', axis=0, tiled=True)]
    dot_general x11 -> x0, matrix products: 29.4 us -> none  [the longest x1 8.14 us: block_step(): jnp.einsum('qk,ke->qe', grad_logits, items_all, preferred_element_type=jn...]
  transfers between devices with their start and end apart: 3 -> 0, of which waited for: 3 -> 0; matrix products, arithmetic and copies ran while one was open for 1% -> 0% of each run, Pallas kernels for 0% -> 0%
where the time goes in v2:
time: 75.4 us; the launch traced here: 75.3 us
  Pallas kernels  74.6 us (99%)
    pallas_call x1, Pallas kernels, step(): pl.pallas_call(functools.partial(kernel, NZ, NY, NX), name='two_tower', o...  72.6 us
    pallas_call x1, Pallas kernels, step(): pl.pallas_call(emit, name='emit', out_shape=[sd((256, 256), f32), sd((256...  2.02 us

profile of v2, /device:TPU:1, one launch (start us, length us, event | category | flops | bytes accessed | tf_op | source)
XLA Modules:
  0.0 75.3 jit_solution(6091189208316215264)
XLA Ops:
  0.6 72.6 %two_tower.1 = (f32[2,2,16,24,128]{4,3,2,1,0:T(8,128)}, f32[1,128]{1,0:T(1,128)}) custom-call(bf16[128,256]{1,0:T(8,128)(2,1)} %qf_h.1, bf16[128,256]{1,0:T(8,128)(2,1)} %vf_h.1, f32[1,128]{1,0:T(1,128)} %bitcast.5, bf16[256,256]{1,0:T(8,128)(2,1)} %wqi_h.1, bf16[256,128]{1,0:T(8,128)(2,1)} %wqo_h.1, bf16[256,256]{1,0:T(8,128)(2,1)} %wvi_h.1, ...), custom_call_target="tpu_custom_call" | custom-call | tf_op jit(solution)/shard_map/two_tower/pallas_call | solution.py:420
  73.3 2.0 %emit.1 = (f32[256,256]{1,0:T(8,128)}, f32[256,128]{1,0:T(8,128)}, f32[256,256]{1,0:T(8,128)}, f32[256,128]{1,0:T(8,128)}, f32[1,128]{1,0:T(1,128)}) custom-call(f32[2,768,128]{2,1,0:T(8,128)} %bitcast.4, f32[1,128]{1,0:T(1,128)} %get-tuple-element.13.loss), custom_call_target="tpu_custom_call" | custom-call | tf_op jit(solution)/shard_map/emit/pallas_call | solution.py:443

commit v3 on v2

--- a/solution.py
+++ b/solution.py
@@ -18,6 +18,7 @@
 NN = (((1,), (0,)), ((), ()))
 R = 128
 GR = 256
+H = R // 2
 
 
 class Scope:
@@ -49,10 +50,10 @@
 
 def kernel(NZ, NY, NX, qf_h, vf_h, lq_h, wqi_h, wqo_h, wvi_h, wvo_h, fin, loss_o,
            qf, vf, lq, wqi, wqo, wvi, wvo, s_in,
-           u_all, v_all, vt, lq_all, bcol, e_all, g_all, csum, stats, invl, invt,
+           u_all, v_all, vt, lq_all, mslot, wslot, cnt, bcol, sbuf, e_all, g_all, csum, stats, invl, invt,
            up, ui, uh, ua, vp, vi, vh, va,
-           su, ru, pv_out, pv_in, sv, rv, gl, gpair, gx_s, gx_r, gz_r, loss_p, loss_x,
-           s_u, r_u, s_v, r_v, s_lq, r_lq, s_st, r_st, s_pv, r_pv, s_sv, r_sv, s_su, r_su,
+           su, ru, hop_in, pv_out, pv_in, sv, rx, ry, tx, ty, r2x, r2y, t_cnt, gl, gpair, gx_s, gx_r, gz_r, loss_p, loss_x,
+           s_u, r_u, s_v, r_v, s_lq, s_st, r_st, s_pv, r_pv, s_p1, s_p2, r_x, r_y, r_2x, r_2y, s_su, r_su, r_hop,
            s_gp, r_gp, s_gx, r_gx, s_gz, r_gz, s_ag, r_ag, s_rl, r_rl, s_lp, r_lp, s_lx, r_lx, s_vr):
     sc = Scope()
     NXY = NY * NX
@@ -102,7 +103,7 @@
     sc("barsig")
     bar = pltpu.get_barrier_semaphore()
     peers = [dev(zs(k, 1), j, c) for k in range(1, NZ)]
-    peers += [dev(z, xs(k, 1), cc) for k in range(1, NXY) for cc in (c, oc)]
+    peers += [dev(z, xs(k, 1), c) for k in range(1, NXY)]
     peers += [dev(z, j, oc)]
     for p in peers:
         pl.semaphore_signal(bar, inc=1, device_id=p, device_id_type=MESH)
@@ -134,81 +135,97 @@
     lq_all[0] = lq[...]
     pos = jnp.sum(u_bf.astype(f32) * v_bf.astype(f32), axis=0, keepdims=True) * (1.0 / TEMP) - lq[...]
     stats[z, :, pl.ds(NQ + 128, 128)] = pos
-    csum[...] = jnp.zeros_like(csum)
 
     sc("barwait")
     pl.semaphore_wait(bar, len(peers))
     sc("sends")
-    mine_u, mine_v = u_all.at[pl.ds(0, R), :], vrows(0)
-    for k in range(1, NXY):
-        for core, cc in ((0, c), (1, oc)):
-            send(lq_all.at[0], lq_all.at[slot(k, core)], s_lq, r_lq, dev(z, xs(k, 1), cc))
-    send(lq_all.at[0], lq_all.at[slot(0, 1)], s_lq, r_lq, dev(z, j, oc))
-    send(mine_v, vrows(slot(0, 1)), s_vr, r_v.at[slot(0, 1)], dev(z, j, oc))
+    mine_u = u_all.at[pl.ds(0, R), :]
+
+    def send_item(s, s2, ss, to):
+        send(lq_all.at[s], lq_all.at[s2], s_lq, r_v.at[s2], to)
+        send(vrows(s), vrows(s2), ss, r_v.at[s2], to)
+
+    send_item(0, slot(0, 1), s_vr, dev(z, j, oc))
     for k in range(1, NXY):
         if k < NZ:
             send(mine_u, u_all.at[pl.ds(k * R, R), :], s_u, r_u.at[k], dev(zs(k, 1), j, c))
-        send(mine_v, vrows(slot(k, 0)), s_v, r_v.at[slot(k, 0)], dev(z, xs(k, 1), c))
-
-    sc("lqwait")
-    wait(lq_all.at[pl.ds(0, 2 * NXY - 1)], r_lq)
-    sc("bias")
-    nl = -lq_all[...].reshape(2 * NXY, 128)
-    m2 = jnp.max(jnp.max(nl, axis=0, keepdims=True), axis=1, keepdims=True) * LOG2E
-    m2 = jnp.broadcast_to(m2, (1, 128))
-    stats[z, :, pl.ds(NQ, 128)] = m2
-    bt = jnp.transpose(m2 - nl * LOG2E)
-    for s in range(2 * NXY):
-        bcol[s * R:(s + 1) * R, :] = jnp.broadcast_to(bt[:, s:s + 1], (R, 128))
-
-    def block(rows, cols):
-        s = dot(v_all[rows, :], u_all[cols, :], NT)
-        b = bcol[rows, :]
-        e = jnp.exp2(s * (LOG2E / TEMP) - jnp.concatenate([b, b], axis=1))
-        e_all[rows, cols] = e
-        csum[:, cols] += jnp.sum(e.reshape(GR // 8, 8, QC), axis=0)
+        send_item(0, slot(k, 0), s_v, dev(z, xs(k, 1), c))
 
     def grp(g):
+        return slice(g * GR, (g + 1) * GR)
+
+    def dyn(g):
         return pl.ds(pl.multiple_of(g * GR, GR), GR)
 
     def qcols(l):
         return slice(l * QC, (l + 1) * QC)
 
-    def new_items(l, g):
-        for l2 in range(l + 1):
-            block(grp(g), qcols(l2))
-        vt[:, grp(g)] = jnp.transpose(v_all[grp(g), :].astype(f32)).astype(bf16)
-
     def loop(lo, n, f):
         lax.fori_loop(0, n, lambda i, u: (f(lo + i), u)[1], 0)
 
-    for l in range(LV):
-        sc(f"uwait{l}")
-        for k in (2 * l, 2 * l + 1):
-            if k:
-                wait(u_all.at[pl.ds(k * R, R), :], r_u.at[k])
-        sc(f"vwait{l}")
-        for k in range(l * SL, (l + 1) * SL):
-            if k:
-                s = slot(k, 0)
-                wait(vrows(s), r_v.at[s])
-                send(vrows(s), vrows(slot(k, 1)), s_vr, r_v.at[slot(k, 1)], dev(z, j, oc))
-        sc(f"pass1_{l}a")
+    def bias(s0):
+        q = lq_all[s0:s0 + SL].reshape(SL, 128)
+        big = jnp.max(-q, axis=1, keepdims=True)
+        b = (big + q) * LOG2E
+        bt = jnp.transpose(jnp.concatenate([b] * (8 // SL), axis=0))
+        for i in range(SL):
+            mslot[s0 + i] = jnp.broadcast_to(big[i:i + 1, :], (1, 128))
+            bcol[(s0 + i) * R:(s0 + i + 1) * R, :] = jnp.broadcast_to(bt[:, i:i + 1], (R, 128))
+
+    def expo(n, g, l):
+        rows, cols = grp(g), qcols(l)
+        bb = bcol[rows, :]
+        e = jnp.exp2(sbuf[n % 2] * (LOG2E / TEMP) - jnp.concatenate([bb, bb], axis=1))
+        e_all[rows, cols] = e
+        csum[2 * g:2 * g + 2, :, cols] = jnp.sum(e.reshape(2, R // 8, 8, QC), axis=1)
+
+    def groups(l, core):
+        return [l * NG + core * (NG // 2) + t for t in range(NG // 2)]
+
+    done = []
+    for l in range(LV + 1):
+        sc(f"wait{l}")
+        fresh = []
+        if l < LV:
+            for k in range(l * SL, (l + 1) * SL):
+                if k:
+                    wait(cnt, r_v.at[slot(k, 0)])
+                    send_item(slot(k, 0), slot(k, 1), s_vr, dev(z, j, oc))
+            for k in (2 * l, 2 * l + 1):
+                if k:
+                    wait(u_all.at[pl.ds(k * R, R), :], r_u.at[k])
+            fresh += groups(l, 0)
         if l:
-            loop(0, l * NG, lambda g: block(grp(g), qcols(l)))
-        sc(f"pass1_{l}b")
-        loop(l * NG, NG // 2, functools.partial(new_items, l))
-        sc(f"vwait{l}p")
-        for k in range(l * SL, (l + 1) * SL):
-            s = slot(k, 1)
-            wait(vrows(s), r_v.at[s])
-        sc(f"pass1_{l}c")
-        loop(l * NG + NG // 2, NG // 2, functools.partial(new_items, l))
+            for k in range((l - 1) * SL, l * SL):
+                wait(cnt, r_v.at[slot(k, 1)])
+            fresh += groups(l - 1, 1)
+        sc(f"pass1_{l}")
+        if l < LV:
+            bias(slot(l * SL, 0))
+        if l:
+            bias(slot((l - 1) * SL, 1))
+        tasks = [(g, l2) for g in fresh for l2 in range(min(l, LV - 1) + 1)]
+        if l < LV:
+            old = [g for g in range(LV * NG) if g in done]
+            tasks = [(g, l) for g in old] + tasks
+        done += fresh
+        for g in fresh:
+            vt[:, grp(g)] = jnp.transpose(v_all[grp(g), :].astype(f32)).astype(bf16)
+        for n, (g, l2) in enumerate(tasks):
+            sbuf[n % 2] = dot(v_all[grp(g), :], u_all[qcols(l2), :], NT)
+            if n:
+                expo(n - 1, *tasks[n - 1])
+        expo(len(tasks) - 1, *tasks[-1])
 
     sc("stats_send")
-    tot = jnp.sum(csum[...], axis=0, keepdims=True)
+    big = jnp.max(mslot[...], axis=0)
+    stats[z, :, pl.ds(NQ, 128)] = big
+    wslot[...] = jnp.exp2((mslot[...] - big) * LOG2E)
     for k in range(NZ):
-        stats[z, :, pl.ds(pl.multiple_of(zs(k, -1) * R, R), R)] = tot[:, k * R:(k + 1) * R]
+        acc = csum[0, :, k * R:(k + 1) * R] * wslot[0]
+        for s in range(1, 2 * NXY):
+            acc = acc + csum[s, :, k * R:(k + 1) * R] * wslot[s]
+        stats[z, :, pl.ds(pl.multiple_of(zs(k, -1) * R, R), R)] = jnp.sum(acc, axis=0, keepdims=True)
     for k in range(1, NZ):
         send(stats.at[z], stats.at[z], s_st, r_st, dev(zs(k, 1), j, c))
     sc("stats_wait")
@@ -218,79 +235,125 @@
     mx = functools.reduce(jnp.maximum, ms)
     tot = jnp.zeros((1, NQ), f32)
     for k in range(NZ):
-        tot = tot + stats[k, :, 0:NQ] * jnp.concatenate([jnp.exp2(ms[k] - mx)] * NZ, axis=1)
-    invt[...] = jnp.concatenate([jnp.exp2(m2 - mx)] * NZ, axis=1) / tot
+        tot = tot + stats[k, :, 0:NQ] * jnp.concatenate([jnp.exp2((ms[k] - mx) * LOG2E)] * NZ, axis=1)
+    invt[...] = jnp.concatenate([jnp.exp2((big - mx) * LOG2E)] * NZ, axis=1) / tot
     for k in range(NZ):
         invl[:, k * R:(k + 1) * R] = invt[:, pl.ds(pl.multiple_of(zs(k, -1) * R, R), R)]
-    lse = (jnp.log2(tot) + jnp.concatenate([mx] * NZ, axis=1)) * LN2
+    lse = jnp.log2(tot) * LN2 + jnp.concatenate([mx] * NZ, axis=1)
     lrow = jnp.zeros((1, 128), f32)
     for k in range(NZ):
         lrow = lrow + (lse[:, k * R:(k + 1) * R] - stats[k, :, NQ + 128:NQ + 256])
     loss_p[c] = lrow
     send(loss_p.at[c], loss_p.at[c], s_lp, r_lp, dev(z, j, oc))
 
-    def norm(rows, c0, c1):
+    def norm(g, c0, c1):
         cols = slice(c0 * QC, c1 * QC)
-        g_all[rows, cols] = (e_all[rows, cols] * invl[:, cols]).astype(bf16)
-
-    def dv(g):
-        return dot(g_all[g * GR:(g + 1) * GR, :], u_all[...])
+        out = []
+        for i in range(2):
+            rows = slice(g * GR + i * R, g * GR + (i + 1) * R)
+            p = e_all[rows, cols] * (invl[:, cols] * jnp.concatenate([wslot[2 * g + i]] * (2 * (c1 - c0)), axis=1))
+            if g == 0 and i == 0 and c0 == 0:
+                col = lax.broadcasted_iota(jnp.int32, p.shape, 1)
+                p = jnp.where(lax.broadcasted_iota(jnp.int32, p.shape, 0) == col, p - 1.0, p)
+            p = p.astype(bf16)
+            g_all[rows, cols] = p
+            out.append(p)
+        return jnp.concatenate(out, axis=0)
 
     pend = []
-
-    def flush():
-        for k in pend:
-            wait(pv_in.at[k], r_pv.at[k])
-            sv[k] = sv[k] + pv_in[k]
-            if k:
-                send(sv.at[k], rv.at[k], s_sv, r_sv, dev(z, xs(k, -1), c))
-        pend.clear()
+    sv_of = {}
+    for k, (a, b) in enumerate(xoff):
+        sv_of[a, b] = k
+
+    def flush(keep):
+        while len(pend) > keep:
+            for k in pend.pop(0):
+                a, b = xoff[k]
+                wait(pv_in.at[k], r_pv.at[k])
+                sv[k] = sv[k] + pv_in[k]
+                if b:
+                    send(sv.at[k, pl.ds(0, H)], rx.at[a, b - 1], s_p1, r_x.at[a], dev(z, xs(sv_of[0, b], -1), c))
+                if a:
+                    send(sv.at[k, pl.ds(H, H)], ry.at[b, a - 1], s_p1, r_y.at[b], dev(z, xs(sv_of[a, 0], -1), c))
 
     def dv_level(l, c0, c1):
         sc(f"dv{l}")
-        for t in range(SL // 2):
-            for core in (1, 0):
-                g = l * NG + core * (NG // 2) + t
-                if c1 > c0:
-                    norm(slice(g * GR, (g + 1) * GR), c0, c1)
-                d = dv(g)
-                ks = (l * SL + 2 * t, l * SL + 2 * t + 1)
-                for i, k in enumerate(ks):
-                    if core:
-                        pv_out[k] = d[i * R:(i + 1) * R, :]
-                        send(pv_out.at[k], pv_in.at[k], s_pv, r_pv.at[k], dev(z, j, oc))
-                    else:
-                        sv[k] = d[i * R:(i + 1) * R, :]
-            flush()
-            pend.extend(ks)
-
-    def du_level(l, nrows):
-        sc(f"du{l}")
-        loop(0, nrows // GR, lambda g: norm(grp(g), l, l + 1))
-        if l == 0:
-            eye = lax.broadcasted_iota(jnp.int32, (R, R), 0) == lax.broadcasted_iota(jnp.int32, (R, R), 1)
-            p = e_all[0:R, 0:R] * invl[:, 0:R]
-            g_all[0:R, 0:R] = jnp.where(eye, p - 1.0, p).astype(bf16)
-        d = dot(vt[...], g_all[:, qcols(l)])
-        for i in range(2):
-            k = 2 * l + i
-            su[k] = d[:, i * R:(i + 1) * R]
-            if k:
-                send(su.at[k], ru.at[k], s_su, r_su, dev(zs(k, -1), j, c))
-
-    dv_level(LV - 1, 0, LV)
-    half = (LV + 1) // 2
-    for l in range(LV - 1, half - 1, -1):
-        du_level(l, (LV - 1) * IR)
-    if LV > 2:
-        dv_level(LV - 2, 0, half)
-    rest = LV - 2 if LV > 2 else LV - 1
-    for l in range(half - 1, -1, -1):
-        du_level(l, rest * IR)
-    for l in range(rest - 1, -1, -1):
-        dv_level(l, 0, 0)
-    sc("flush")
-    flush()
+        ks = list(range(l * SL, (l + 1) * SL))
+        for g in range(l * NG, (l + 1) * NG):
+            if c1 > c0:
+                norm(g, c0, c1)
+        d = dot(g_all[l * IR:(l + 1) * IR, :], u_all[...])
+        for i, k in enumerate(ks):
+            pv_out[k] = d[(SL + i) * R:(SL + i + 1) * R, :]
+            send(pv_out.at[k], pv_in.at[k], s_pv, r_pv.at[k], dev(z, j, oc))
+            sv[k] = d[i * R:(i + 1) * R, :]
+        flush(0)
+        pend.append(ks)
+
+    def du_levels(l0, l1, fresh):
+        sc(f"du{l0}")
+        d = None
+        for lk in range(LV):
+            if lk < fresh:
+                gv = jnp.concatenate([norm(g, l0, l1) for g in range(lk * NG, (lk + 1) * NG)], axis=0)
+            else:
+                gv = g_all[lk * IR:(lk + 1) * IR, l0 * QC:l1 * QC]
+            p = dot(vt[:, lk * IR:(lk + 1) * IR], gv)
+            d = p if d is None else d + p
+        for k in range(2 * l0, 2 * l1):
+            su[k] = d[:, (k - 2 * l0) * R:(k - 2 * l0 + 1) * R]
+        for k in range(2 * l0, 2 * l1):
+            if k and k not in late:
+                send_u(k, near.get(k, zoff[k]))
+
+    near, late = {}, {}
+    if NZ >= 99:
+        for o, via in ((3, 2), (NZ - 3, NZ - 2)):
+            near[zoff.index(o)] = (o - via) % NZ
+            late[zoff.index(via)] = zoff.index(o)
+
+    def send_u(k, hop):
+        to = lax.rem(z + (NZ - hop), NZ)
+        sem = r_hop.at[k] if k in near else r_su
+        dst = hop_in.at[k] if k in near else ru.at[k]
+        send(su.at[k], dst, s_su, sem, dev(to, j, c))
+
+    def send_late(k):
+        sc("late")
+        wait(hop_in.at[late[k]], r_hop.at[late[k]])
+        su[k] = su[k] + hop_in[late[k]]
+        send_u(k, zoff[k])
+
+    if LV == 4:
+        du_levels(3, 4, 4)
+        dv_level(3, 0, 3)
+        dv_level(2, 0, 3)
+        du_levels(2, 3, 2)
+        dv_level(1, 0, 2)
+        dv_level(0, 0, 2)
+        du_levels(1, 2, 0)
+        flush(0)
+        du_levels(0, 1, 0)
+    else:
+        du_levels(1, 2, 2)
+        dv_level(1, 0, 1)
+        dv_level(0, 0, 1)
+        du_levels(0, 1, 0)
+        flush(0)
+
+    def leg2(n, own, r1, sem1, t1, r2, sem2, far):
+        for o in ring(n)[::-1]:
+            wait(r1.at[o], sem1.at[o])
+            acc = own(o)
+            for i in range(r1.shape[1]):
+                acc = acc + r1[o, i]
+            t1[o] = acc
+            if o:
+                send(t1.at[o], r2.at[o - 1], s_p2, sem2, far(o))
+
+    sc("leg2")
+    leg2(NY, lambda a: sv[sv_of[a, 0], 0:H], rx, r_x, tx, r2x, r_2x, lambda a: dev(z, xs(sv_of[a, 0], -1), c))
+    leg2(NX, lambda b: sv[sv_of[0, b], H:R], ry, r_y, ty, r2y, r_2y, lambda b: dev(z, xs(sv_of[0, b], -1), c))
 
     sc("loss")
     wait(loss_p.at[oc], r_lp)
@@ -348,28 +411,32 @@
             send(ref, ref, s_rl.at[t], r_rl.at[t, k], dev(z, j, oc))
 
     scale = 1.0 / (TEMP * B)
+    sc("rv_wait")
+    wait(r2x, r_2x)
+    wait(r2y, r_2y)
+    sc("bwd_v")
+    top, bot = tx[0], ty[0]
+    for i in range(NY - 1):
+        top = top + r2x[i]
+    for i in range(NX - 1):
+        bot = bot + r2y[i]
+    backward(jnp.concatenate([top, bot], axis=0) * scale, vf, wvo, vp, vi, vh, va, 1)
+    pair_sum(1)
     sc("ru_wait")
-    wait(ru.at[pl.ds(0, NZ - 1)], r_su)
+    wait(ru.at[pl.ds(0, NZ - 1 - len(near))], r_su)
     sc("bwd_q")
     acc = su[0]
     for k in range(1, NZ):
-        acc = acc + ru[k]
+        if k not in near:
+            acc = acc + ru[k]
     backward(jnp.transpose(acc) * scale, qf, wqo, up, ui, uh, ua, 0)
     pair_sum(0)
-    sc("rv_wait")
-    wait(rv.at[pl.ds(0, NXY - 1)], r_sv)
-    sc("bwd_v")
-    acc = sv[0]
-    for k in range(1, NXY):
-        acc = acc + rv[k]
-    backward(acc * scale, vf, wvo, vp, vi, vh, va, 1)
-    pair_sum(1)
+    plane_sum(1)
     plane_sum(0)
-    plane_sum(1)
+    ring_sum(1)
     ring_sum(0)
-    ring_sum(1)
+    relay(1)
     relay(0)
-    relay(1)
     sc("loss2")
     wait(loss_x.at[pl.ds(0, NXY - 1)], r_lx)
     ls = loss_x[0]
@@ -389,7 +456,8 @@
     wait(stats.at[pl.ds(0, NZ - 1)], s_st)
     wait(loss_p.at[0], s_lp)
     wait(pv_out, s_pv)
-    wait(sv.at[pl.ds(0, NXY - 1)], s_sv)
+    wait(sv.at[pl.ds(0, (NY * (NX - 1) + NX * (NY - 1)) // 2)], s_p1)
+    wait(t_cnt, s_p2)
     wait(su.at[pl.ds(0, NZ - 1)], s_su)
     wait(loss_x.at[pl.ds(0, NXY - 1)], s_lx)
     for t in range(2):
@@ -426,15 +494,17 @@
             scratch_shapes=[
                 V((R, 256), bf16), V((R, 256), bf16), V((1, 128), f32),
                 V((256, 256), bf16), V((256, 128), bf16), V((256, 256), bf16), V((256, 128), bf16), S((7,)),
-                V((NQ, 128), bf16), V((NI, 128), bf16), V((128, NI), bf16), V((2 * NXY, 1, 128), f32),
-                V((NI, 128), f32), V((NI, NQ), f32), V((NI, NQ), bf16), V((8, NQ), f32),
+                V((NQ, 128), bf16), V((NI, 128), bf16), V((128, NI), bf16), V((2 * NXY, 1, 128), f32), V((2 * NXY, 1, 128), f32), V((2 * NXY, 1, 128), f32), V((65, 1, 128), f32),
+                V((NI, 128), f32), V((2, GR, 2 * R), f32), V((NI, NQ), f32), V((NI, NQ), bf16), V((2 * NXY, 8, NQ), f32),
                 V((NZ, 1, NQ + 256), f32), V((1, NQ), f32), V((1, NQ), f32),
                 *tower, *tower,
-                V((NZ, 128, 128), f32), V((NZ, 128, 128), f32),
-                V((NXY, 128, 128), f32), V((NXY, 128, 128), f32), V((NXY, 128, 128), f32), V((NXY, 128, 128), f32),
+                V((NZ, 128, 128), f32), V((NZ, 128, 128), f32), V((NZ, 128, 128), f32),
+                V((NXY, 128, 128), f32), V((NXY, 128, 128), f32), V((NXY, 128, 128), f32),
+                V((NY, NX - 1, H, 128), f32), V((NX, NY - 1, H, 128), f32), V((NY, H, 128), f32), V((NX, H, 128), f32),
+                V((NY - 1, H, 128), f32), V((NX - 1, H, 128), f32), V((NY + NX - 2, H, 128), f32),
                 V((2, 768, 128), f32), V((2, 384, 128), f32), V((2, NXY, CH, 128), f32), V((2, NXY, CH, 128), f32),
                 V((2, NZ, CH, 128), f32), V((2, 1, 128), f32), V((NXY, 1, 128), f32),
-                S, S((NZ,)), S, S((2 * NXY,)), S, S, S, S, S, S((NXY,)), S, S, S, S,
+                S, S((NZ,)), S, S((2 * NXY,)), S, S, S, S, S((NXY,)), S, S, S((NY,)), S((NX,)), S, S, S, S, S((NZ,)),
                 S((2,)), S((2,)), S((2,)), S((2,)), S((2,)), S((2,)), S((2,)), S((2, NXY)), S((2,)), S((2, NXY)),
                 S, S, S, S, S,
             ],

time: 75.4 us -> 69.7 us (0.924)
  Pallas kernels: 74.6 us -> 68.9 us
    pallas_call x1, Pallas kernels: 72.6 us -> 66.9 us  [step(): pl.pallas_call(functools.partial(kernel, NZ, NY, NX), name='two_tower', o...]
where the time goes in v3:
time: 69.7 us; the launch traced here: 69.5 us
  Pallas kernels  68.9 us (99%)
    pallas_call x1, Pallas kernels, step(): pl.pallas_call(functools.partial(kernel, NZ, NY, NX), name='two_tower', o...  66.9 us
    pallas_call x1, Pallas kernels, step(): pl.pallas_call(emit, name='emit', out_shape=[sd((256, 256), f32), sd((256...  2.02 us

profile of v3, /device:TPU:1, one launch (start us, length us, event | category | flops | bytes accessed | tf_op | source)
XLA Modules:
  0.0 69.5 jit_solution(9019046882882207175)
XLA Ops:
  0.6 66.9 %two_tower.1 = (f32[2,2,16,24,128]{4,3,2,1,0:T(8,128)}, f32[1,128]{1,0:T(1,128)}) custom-call(bf16[128,256]{1,0:T(8,128)(2,1)} %qf_h.1, bf16[128,256]{1,0:T(8,128)(2,1)} %vf_h.1, f32[1,128]{1,0:T(1,128)} %bitcast.5, bf16[256,256]{1,0:T(8,128)(2,1)} %wqi_h.1, bf16[256,128]{1,0:T(8,128)(2,1)} %wqo_h.1, bf16[256,256]{1,0:T(8,128)(2,1)} %wvi_h.1, ...), custom_call_target="tpu_custom_call" | custom-call | tf_op jit(solution)/shard_map/two_tower/pallas_call | solution.py:488
  67.5 2.0 %emit.1 = (f32[256,256]{1,0:T(8,128)}, f32[256,128]{1,0:T(8,128)}, f32[256,256]{1,0:T(8,128)}, f32[256,128]{1,0:T(8,128)}, f32[1,128]{1,0:T(1,128)}) custom-call(f32[2,768,128]{2,1,0:T(8,128)} %bitcast.4, f32[1,128]{1,0:T(1,128)} %get-tuple-element.13.loss), custom_call_target="tpu_custom_call" | custom-call | tf_op jit(solution)/shard_map/emit/pallas_call | solution.py:513

commit v4 on v3

--- a/solution.py
+++ b/solution.py
@@ -38,6 +38,11 @@
     return lax.dot_general(a, b, dims, preferred_element_type=f32)
 
 
+def arrange(near, level):
+    rest = near[level:]
+    return near[:level] + rest[level:][::-1] + rest[:level]
+
+
 def ring(n):
     return sorted(range(n), key=lambda k: (min(k, n - k), k))
 
@@ -45,15 +50,15 @@
 def torus(ny, nx):
     def dist(o):
         return min(o[0], ny - o[0]) + min(o[1], nx - o[1])
-    return sorted(((a, b) for a in range(ny) for b in range(nx)), key=lambda o: (dist(o), o))
+    return sorted(((a, b) for a in range(ny) for b in range(nx)), key=lambda o: (dist(o), o[0] * o[1] != 0, o))
 
 
 def kernel(NZ, NY, NX, qf_h, vf_h, lq_h, wqi_h, wqo_h, wvi_h, wvo_h, fin, loss_o,
            qf, vf, lq, wqi, wqo, wvi, wvo, s_in,
            u_all, v_all, vt, lq_all, mslot, wslot, cnt, bcol, sbuf, e_all, g_all, csum, stats, invl, invt,
            up, ui, uh, ua, vp, vi, vh, va,
-           su, ru, hop_in, pv_out, pv_in, sv, rx, ry, tx, ty, r2x, r2y, t_cnt, gl, gpair, gx_s, gx_r, gz_r, loss_p, loss_x,
-           s_u, r_u, s_v, r_v, s_lq, s_st, r_st, s_pv, r_pv, s_p1, s_p2, r_x, r_y, r_2x, r_2y, s_su, r_su, r_hop,
+           su, ru, pv_out, pv_in, sv, rx, ry, tx, ty, r2x, r2y, t_cnt, gl, gpair, gx_s, gx_r, gz_r, loss_p, loss_x,
+           s_u, r_u, s_v, r_v, s_lq, s_st, r_st, s_pv, r_pv, s_p1, s_p2, r_x, r_y, r_2x, r_2y, s_su, r_su,
            s_gp, r_gp, s_gx, r_gx, s_gz, r_gz, s_ag, r_ag, s_rl, r_rl, s_lp, r_lp, s_lx, r_lx, s_vr):
     sc = Scope()
     NXY = NY * NX
@@ -66,7 +71,9 @@
     QC = 2 * R
     IR = 2 * SL * R
     NG = IR // GR
-    zoff, xoff = ring(NZ), torus(NY, NX)
+    zoff, xoff = arrange(ring(NZ), 2), arrange(torus(NY, NX), SL)
+    zfar = [zoff.index(o) for o in ring(NZ)[:0:-1]]
+    xfar = [xoff.index(o) for o in torus(NY, NX)[:0:-1]]
     me = lax.axis_index("dp")
     c = lax.rem(me, 2)
     j = lax.rem(lax.div(me, 2), NXY)
@@ -226,7 +233,7 @@
         for s in range(1, 2 * NXY):
             acc = acc + csum[s, :, k * R:(k + 1) * R] * wslot[s]
         stats[z, :, pl.ds(pl.multiple_of(zs(k, -1) * R, R), R)] = jnp.sum(acc, axis=0, keepdims=True)
-    for k in range(1, NZ):
+    for k in zfar:
         send(stats.at[z], stats.at[z], s_st, r_st, dev(zs(k, 1), j, c))
     sc("stats_wait")
     wait(stats.at[pl.ds(0, NZ - 1)], r_st)
@@ -276,84 +283,81 @@
                 if a:
                     send(sv.at[k, pl.ds(H, H)], ry.at[b, a - 1], s_p1, r_y.at[b], dev(z, xs(sv_of[a, 0], -1), c))
 
-    def dv_level(l, c0, c1):
-        sc(f"dv{l}")
-        ks = list(range(l * SL, (l + 1) * SL))
-        for g in range(l * NG, (l + 1) * NG):
-            if c1 > c0:
-                norm(g, c0, c1)
-        d = dot(g_all[l * IR:(l + 1) * IR, :], u_all[...])
-        for i, k in enumerate(ks):
-            pv_out[k] = d[(SL + i) * R:(SL + i + 1) * R, :]
-            send(pv_out.at[k], pv_in.at[k], s_pv, r_pv.at[k], dev(z, j, oc))
-            sv[k] = d[i * R:(i + 1) * R, :]
-        flush(0)
-        pend.append(ks)
-
-    def du_levels(l0, l1, fresh):
-        sc(f"du{l0}")
-        d = None
-        for lk in range(LV):
-            if lk < fresh:
-                gv = jnp.concatenate([norm(g, l0, l1) for g in range(lk * NG, (lk + 1) * NG)], axis=0)
+    normed = set()
+
+    def ready(g, l):
+        if (g, l) not in normed:
+            normed.add((g, l))
+            norm(g, l, l + 1)
+
+    def dv_half(ls, core):
+        sc(f"dv{ls[0]}{core}")
+        ds = []
+        for l in ls:
+            gs = groups(l, core)
+            for g in gs:
+                for l2 in range(LV):
+                    ready(g, l2)
+            ds.append(dot(g_all[gs[0] * GR:(gs[-1] + 1) * GR, :], u_all[...]))
+        keep = pv_out if core else sv
+        for l, d in zip(ls, ds):
+            for i in range(SL):
+                keep[l * SL + i] = d[i * R:(i + 1) * R, :]
+        for l in ls:
+            ks = list(range(l * SL, (l + 1) * SL))
+            if core:
+                for k in ks:
+                    send(pv_out.at[k], pv_in.at[k], s_pv, r_pv.at[k], dev(z, j, oc))
             else:
-                gv = g_all[lk * IR:(lk + 1) * IR, l0 * QC:l1 * QC]
-            p = dot(vt[:, lk * IR:(lk + 1) * IR], gv)
-            d = p if d is None else d + p
-        for k in range(2 * l0, 2 * l1):
-            su[k] = d[:, (k - 2 * l0) * R:(k - 2 * l0 + 1) * R]
-        for k in range(2 * l0, 2 * l1):
-            if k and k not in late:
-                send_u(k, near.get(k, zoff[k]))
-
-    near, late = {}, {}
-    if NZ >= 99:
-        for o, via in ((3, 2), (NZ - 3, NZ - 2)):
-            near[zoff.index(o)] = (o - via) % NZ
-            late[zoff.index(via)] = zoff.index(o)
-
-    def send_u(k, hop):
-        to = lax.rem(z + (NZ - hop), NZ)
-        sem = r_hop.at[k] if k in near else r_su
-        dst = hop_in.at[k] if k in near else ru.at[k]
-        send(su.at[k], dst, s_su, sem, dev(to, j, c))
-
-    def send_late(k):
-        sc("late")
-        wait(hop_in.at[late[k]], r_hop.at[late[k]])
-        su[k] = su[k] + hop_in[late[k]]
-        send_u(k, zoff[k])
+                pend.append(ks)
+        if not core:
+            sc(f"flush{ls[0]}")
+            flush(0)
+
+    def du_levels(ls):
+        sc(f"du{ls[0]}")
+        for l in ls:
+            parts = []
+            for lk in range(LV):
+                for g in range(lk * NG, (lk + 1) * NG):
+                    ready(g, l)
+                rows = slice(lk * IR, (lk + 1) * IR)
+                parts.append(dot(vt[:, rows], g_all[rows, qcols(l)]))
+            d = functools.reduce(jnp.add, parts)
+            for i in range(2):
+                su[2 * l + i] = d[:, i * R:(i + 1) * R]
+        for l in ls:
+            for k in (2 * l, 2 * l + 1):
+                if k:
+                    send(su.at[k], ru.at[k], s_su, r_su, dev(zs(k, -1), j, c))
 
     if LV == 4:
-        du_levels(3, 4, 4)
-        dv_level(3, 0, 3)
-        dv_level(2, 0, 3)
-        du_levels(2, 3, 2)
-        dv_level(1, 0, 2)
-        dv_level(0, 0, 2)
-        du_levels(1, 2, 0)
-        flush(0)
-        du_levels(0, 1, 0)
+        dv_half([1, 2], 1)
+        du_levels([1, 2])
+        dv_half([1, 2], 0)
+        dv_half([3, 0], 1)
+        du_levels([3, 0])
+        dv_half([3, 0], 0)
     else:
-        du_levels(1, 2, 2)
-        dv_level(1, 0, 1)
-        dv_level(0, 0, 1)
-        du_levels(0, 1, 0)
-        flush(0)
-
-    def leg2(n, own, r1, sem1, t1, r2, sem2, far):
-        for o in ring(n)[::-1]:
-            wait(r1.at[o], sem1.at[o])
-            acc = own(o)
-            for i in range(r1.shape[1]):
-                acc = acc + r1[o, i]
-            t1[o] = acc
-            if o:
-                send(t1.at[o], r2.at[o - 1], s_p2, sem2, far(o))
+        dv_half([0, 1], 1)
+        du_levels([1, 0])
+        dv_half([0, 1], 0)
+
+    def leg2(o, own, r1, sem1, t1, r2, sem2, far):
+        wait(r1.at[o], sem1.at[o])
+        acc = own
+        for i in range(r1.shape[1]):
+            acc = acc + r1[o, i]
+        t1[o] = acc
+        if o:
+            send(t1.at[o], r2.at[o - 1], s_p2, sem2, far)
 
     sc("leg2")
-    leg2(NY, lambda a: sv[sv_of[a, 0], 0:H], rx, r_x, tx, r2x, r_2x, lambda a: dev(z, xs(sv_of[a, 0], -1), c))
-    leg2(NX, lambda b: sv[sv_of[0, b], H:R], ry, r_y, ty, r2y, r_2y, lambda b: dev(z, xs(sv_of[0, b], -1), c))
+    for o in ring(max(NY, NX))[::-1]:
+        if o < NY:
+            leg2(o, sv[sv_of[o, 0], 0:H], rx, r_x, tx, r2x, r_2x, dev(z, xs(sv_of[o, 0], -1), c))
+        if o < NX:
+            leg2(o, sv[sv_of[0, o], H:R], ry, r_y, ty, r2y, r_2y, dev(z, xs(sv_of[0, o], -1), c))
 
     sc("loss")
     wait(loss_p.at[oc], r_lp)
@@ -377,7 +381,7 @@
         sc(f"gp_wait{t}")
         wait(gpair.at[t], r_gp.at[t])
         gx_s[t] = (gl[t, pl.ds(pl.multiple_of(c * 384, 8), 384), :] + gpair[t]).reshape(NXY, CH, 128)
-        for k in range(1, NXY):
+        for k in xfar:
             to = xs(k, 1)
             send(gx_s.at[t, to], gx_r.at[t, j], s_gx.at[t], r_gx.at[t], dev(z, to, c))
         gx_r[t, j] = gx_s[t, j]
@@ -389,7 +393,7 @@
         for k in range(1, NXY):
             acc = acc + gx_r[t, k]
         gz_r[t, z] = acc
-        for k in range(1, NZ):
+        for k in zfar:
             send(gz_r.at[t, z], gz_r.at[t, z], s_gz.at[t], r_gz.at[t], dev(zs(k, 1), j, c))
 
     def ring_sum(t):
@@ -399,13 +403,13 @@
         for k in range(1, NZ):
             acc = acc + gz_r[t, k]
         fin[t, c, j] = acc
-        for k in range(1, NXY):
+        for k in xfar:
             send(fin.at[t, c, j], fin.at[t, c, j], s_ag.at[t], r_ag.at[t, k], dev(z, xs(k, 1), c))
         send(fin.at[t, c, j], fin.at[t, c, j], s_rl.at[t], r_rl.at[t, 0], dev(z, j, oc))
 
     def relay(t):
         sc(f"ag_wait{t}")
-        for k in range(1, NXY):
+        for k in xfar:
             ref = fin.at[t, c, xs(k, -1)]
             wait(ref, r_ag.at[t, k])
             send(ref, ref, s_rl.at[t], r_rl.at[t, k], dev(z, j, oc))
@@ -423,12 +427,11 @@
     backward(jnp.concatenate([top, bot], axis=0) * scale, vf, wvo, vp, vi, vh, va, 1)
     pair_sum(1)
     sc("ru_wait")
-    wait(ru.at[pl.ds(0, NZ - 1 - len(near))], r_su)
+    wait(ru.at[pl.ds(0, NZ - 1)], r_su)
     sc("bwd_q")
     acc = su[0]
     for k in range(1, NZ):
-        if k not in near:
-            acc = acc + ru[k]
+        acc = acc + ru[k]
     backward(jnp.transpose(acc) * scale, qf, wqo, up, ui, uh, ua, 0)
     pair_sum(0)
     plane_sum(1)
@@ -498,13 +501,13 @@
                 V((NI, 128), f32), V((2, GR, 2 * R), f32), V((NI, NQ), f32), V((NI, NQ), bf16), V((2 * NXY, 8, NQ), f32),
                 V((NZ, 1, NQ + 256), f32), V((1, NQ), f32), V((1, NQ), f32),
                 *tower, *tower,
-                V((NZ, 128, 128), f32), V((NZ, 128, 128), f32), V((NZ, 128, 128), f32),
+                V((NZ, 128, 128), f32), V((NZ, 128, 128), f32),
                 V((NXY, 128, 128), f32), V((NXY, 128, 128), f32), V((NXY, 128, 128), f32),
                 V((NY, NX - 1, H, 128), f32), V((NX, NY - 1, H, 128), f32), V((NY, H, 128), f32), V((NX, H, 128), f32),
                 V((NY - 1, H, 128), f32), V((NX - 1, H, 128), f32), V((NY + NX - 2, H, 128), f32),
                 V((2, 768, 128), f32), V((2, 384, 128), f32), V((2, NXY, CH, 128), f32), V((2, NXY, CH, 128), f32),
                 V((2, NZ, CH, 128), f32), V((2, 1, 128), f32), V((NXY, 1, 128), f32),
-                S, S((NZ,)), S, S((2 * NXY,)), S, S, S, S, S((NXY,)), S, S, S((NY,)), S((NX,)), S, S, S, S, S((NZ,)),
+                S, S((NZ,)), S, S((2 * NXY,)), S, S, S, S, S((NXY,)), S, S, S((NY,)), S((NX,)), S, S, S, S,
                 S((2,)), S((2,)), S((2,)), S((2,)), S((2,)), S((2,)), S((2,)), S((2, NXY)), S((2,)), S((2, NXY)),
                 S, S, S, S, S,
             ],

time: 69.7 us -> 65.3 us (0.937)
  Pallas kernels: 68.9 us -> 64.6 us
    pallas_call x1, Pallas kernels: 66.9 us -> 62.5 us  [step(): pl.pallas_call(functools.partial(kernel, NZ, NY, NX), name='two_tower', o...]
where the time goes in v4:
time: 65.3 us; the launch traced here: 65.2 us
  Pallas kernels  64.6 us (99%)
    pallas_call x1, Pallas kernels, step(): pl.pallas_call(functools.partial(kernel, NZ, NY, NX), name='two_tower', o...  62.5 us
    pallas_call x1, Pallas kernels, step(): pl.pallas_call(emit, name='emit', out_shape=[sd((256, 256), f32), sd((256...  2.02 us

profile of v4, /device:TPU:1, one launch (start us, length us, event | category | flops | bytes accessed | tf_op | source)
XLA Modules:
  0.0 65.2 jit_solution(15822968189133677609)
XLA Ops:
  0.6 62.5 %two_tower.1 = (f32[2,2,16,24,128]{4,3,2,1,0:T(8,128)}, f32[1,128]{1,0:T(1,128)}) custom-call(bf16[128,256]{1,0:T(8,128)(2,1)} %qf_h.1, bf16[128,256]{1,0:T(8,128)(2,1)} %vf_h.1, f32[1,128]{1,0:T(1,128)} %bitcast.5, bf16[256,256]{1,0:T(8,128)(2,1)} %wqi_h.1, bf16[256,128]{1,0:T(8,128)(2,1)} %wqo_h.1, bf16[256,256]{1,0:T(8,128)(2,1)} %wvi_h.1, ...), custom_call_target="tpu_custom_call" | custom-call | tf_op jit(solution)/shard_map/two_tower/pallas_call | solution.py:491
  63.2 2.0 %emit.1 = (f32[256,256]{1,0:T(8,128)}, f32[256,128]{1,0:T(8,128)}, f32[256,256]{1,0:T(8,128)}, f32[256,128]{1,0:T(8,128)}, f32[1,128]{1,0:T(1,128)}) custom-call(f32[2,768,128]{2,1,0:T(8,128)} %bitcast.4, f32[1,128]{1,0:T(1,128)} %get-tuple-element.13.loss), custom_call_target="tpu_custom_call" | custom-call | tf_op jit(solution)/shard_map/emit/pallas_call | solution.py:516

commit v5 on v4

--- a/solution.py
+++ b/solution.py
@@ -57,8 +57,8 @@
            qf, vf, lq, wqi, wqo, wvi, wvo, s_in,
            u_all, v_all, vt, lq_all, mslot, wslot, cnt, bcol, sbuf, e_all, g_all, csum, stats, invl, invt,
            up, ui, uh, ua, vp, vi, vh, va,
-           su, ru, pv_out, pv_in, sv, rx, ry, tx, ty, r2x, r2y, t_cnt, gl, gpair, gx_s, gx_r, gz_r, loss_p, loss_x,
-           s_u, r_u, s_v, r_v, s_lq, s_st, r_st, s_pv, r_pv, s_p1, s_p2, r_x, r_y, r_2x, r_2y, s_su, r_su,
+           su, ru, hop_in, pv_out, pv_in, sv, rx, ry, tx, ty, r2x, r2y, t_cnt, gl, gpair, gx_s, gx_r, gz_r, loss_p, loss_x,
+           s_u, r_u, s_v, r_v, s_lq, s_st, r_st, s_pv, r_pv, s_p1, s_p2, r_x, r_y, r_2x, r_2y, s_su, r_su, r_hop,
            s_gp, r_gp, s_gx, r_gx, s_gz, r_gz, s_ag, r_ag, s_rl, r_rl, s_lp, r_lp, s_lx, r_lx, s_vr):
     sc = Scope()
     NXY = NY * NX
@@ -115,17 +115,16 @@
     for p in peers:
         pl.semaphore_signal(bar, inc=1, device_id=p, device_id_type=MESH)
     loads = [pltpu.make_async_copy(a, b, s_in.at[i]) for i, (a, b) in enumerate(
-        ((qf_h, qf), (wqi_h, wqi), (wqo_h, wqo), (vf_h, vf), (wvi_h, wvi), (wvo_h, wvo), (lq_h, lq)))]
+        ((vf_h, vf), (wvi_h, wvi), (wvo_h, wvo), (lq_h, lq), (qf_h, qf), (wqi_h, wqi), (wqo_h, wqo)))]
     for cp in loads:
         cp.start()
-    for cp in loads:
-        cp.wait()
-
-    sc("tower")
-
-    def tower(xr, wi, wo, unit, inv, hid, act):
+
+    def tower(xr, wi, wo, unit, inv, hid, act, cps):
+        cps[0].wait()
+        cps[1].wait()
         a = dot(xr[...], wi[...])
         h = jnp.maximum(a, 0.0).astype(bf16)
+        cps[2].wait()
         e = dot(h, wo[...])
         r = lax.rsqrt(jnp.sum(e * e, axis=-1, keepdims=True) + EPS)
         u = e * r
@@ -135,28 +134,28 @@
         act[...] = a
         return u.astype(bf16)
 
-    u_bf = tower(qf, wqi, wqo, up, ui, uh, ua)
-    v_bf = tower(vf, wvi, wvo, vp, vi, vh, va)
-    u_all[0:R, :] = u_bf
-    v_all[0:R, :] = v_bf
-    lq_all[0] = lq[...]
-    pos = jnp.sum(u_bf.astype(f32) * v_bf.astype(f32), axis=0, keepdims=True) * (1.0 / TEMP) - lq[...]
-    stats[z, :, pl.ds(NQ + 128, 128)] = pos
-
-    sc("barwait")
-    pl.semaphore_wait(bar, len(peers))
-    sc("sends")
-    mine_u = u_all.at[pl.ds(0, R), :]
-
     def send_item(s, s2, ss, to):
         send(lq_all.at[s], lq_all.at[s2], s_lq, r_v.at[s2], to)
         send(vrows(s), vrows(s2), ss, r_v.at[s2], to)
 
+    sc("tower_v")
+    v_bf = tower(vf, wvi, wvo, vp, vi, vh, va, loads[0:3])
+    v_all[0:R, :] = v_bf
+    loads[3].wait()
+    lq_all[0] = lq[...]
+    sc("barwait")
+    pl.semaphore_wait(bar, len(peers))
+    sc("sends_v")
+    for k in range(1, NXY):
+        send_item(0, slot(k, 0), s_v, dev(z, xs(k, 1), c))
     send_item(0, slot(0, 1), s_vr, dev(z, j, oc))
-    for k in range(1, NXY):
-        if k < NZ:
-            send(mine_u, u_all.at[pl.ds(k * R, R), :], s_u, r_u.at[k], dev(zs(k, 1), j, c))
-        send_item(0, slot(k, 0), s_v, dev(z, xs(k, 1), c))
+    sc("tower_q")
+    u_bf = tower(qf, wqi, wqo, up, ui, uh, ua, loads[4:7])
+    u_all[0:R, :] = u_bf
+    for k in range(1, NZ):
+        send(u_all.at[pl.ds(0, R), :], u_all.at[pl.ds(k * R, R), :], s_u, r_u.at[k], dev(zs(k, 1), j, c))
+    pos = jnp.sum(u_bf.astype(f32) * v_bf.astype(f32), axis=0, keepdims=True) * (1.0 / TEMP) - lq[...]
+    stats[z, :, pl.ds(NQ + 128, 128)] = pos
 
     def grp(g):
         return slice(g * GR, (g + 1) * GR)
@@ -216,8 +215,6 @@
             old = [g for g in range(LV * NG) if g in done]
             tasks = [(g, l) for g in old] + tasks
         done += fresh
-        for g in fresh:
-            vt[:, grp(g)] = jnp.transpose(v_all[grp(g), :].astype(f32)).astype(bf16)
         for n, (g, l2) in enumerate(tasks):
             sbuf[n % 2] = dot(v_all[grp(g), :], u_all[qcols(l2), :], NT)
             if n:
@@ -235,6 +232,9 @@
         stats[z, :, pl.ds(pl.multiple_of(zs(k, -1) * R, R), R)] = jnp.sum(acc, axis=0, keepdims=True)
     for k in zfar:
         send(stats.at[z], stats.at[z], s_st, r_st, dev(zs(k, 1), j, c))
+    sc("transpose")
+    for g in range(LV * NG):
+        vt[:, grp(g)] = jnp.transpose(v_all[grp(g), :].astype(f32)).astype(bf16)
     sc("stats_wait")
     wait(stats.at[pl.ds(0, NZ - 1)], r_st)
     sc("stats_comp")
@@ -298,11 +298,12 @@
             for g in gs:
                 for l2 in range(LV):
                     ready(g, l2)
-            ds.append(dot(g_all[gs[0] * GR:(gs[-1] + 1) * GR, :], u_all[...]))
+            rows = [(gs[0] * GR, (gs[-1] + 1) * GR)] if len(ls) > 1 else [(g * GR, (g + 1) * GR) for g in gs]
+            ds += [(l, r0 - gs[0] * GR, dot(g_all[r0:r1, :], u_all[...])) for r0, r1 in rows]
         keep = pv_out if core else sv
-        for l, d in zip(ls, ds):
-            for i in range(SL):
-                keep[l * SL + i] = d[i * R:(i + 1) * R, :]
+        for l, r0, d in ds:
+            for i in range(d.shape[0] // R):
+                keep[l * SL + r0 // R + i] = d[i * R:(i + 1) * R, :]
         for l in ls:
             ks = list(range(l * SL, (l + 1) * SL))
             if core:
@@ -326,10 +327,26 @@
             d = functools.reduce(jnp.add, parts)
             for i in range(2):
                 su[2 * l + i] = d[:, i * R:(i + 1) * R]
-        for l in ls:
-            for k in (2 * l, 2 * l + 1):
-                if k:
-                    send(su.at[k], ru.at[k], s_su, r_su, dev(zs(k, -1), j, c))
+        ks = [k for l in ls for k in (2 * l, 2 * l + 1)]
+        for k in ks:
+            if k in hop:
+                send(su.at[k], hop_in.at[k], s_su, r_hop.at[k], dev(lax.rem(z + NZ - hop[k], NZ), j, c))
+        for k in ks:
+            if k and k not in hop and k not in late:
+                send(su.at[k], ru.at[k], s_su, r_su, dev(zs(k, -1), j, c))
+
+    hop, late = {}, {}
+    if NZ >= 8:
+        for o, via in ((3, 2), (NZ - 3, NZ - 2)):
+            hop[zoff.index(o)] = (o - via) % NZ
+            late[zoff.index(via)] = zoff.index(o)
+
+    def send_late():
+        sc("late")
+        for k, k2 in late.items():
+            wait(hop_in.at[k2], r_hop.at[k2])
+            su[k] = su[k] + hop_in[k2]
+            send(su.at[k], ru.at[k], s_su, r_su, dev(zs(k, -1), j, c))
 
     if LV == 4:
         dv_half([1, 2], 1)
@@ -338,6 +355,7 @@
         dv_half([3, 0], 1)
         du_levels([3, 0])
         dv_half([3, 0], 0)
+        send_late()
     else:
         dv_half([0, 1], 1)
         du_levels([1, 0])
@@ -427,11 +445,12 @@
     backward(jnp.concatenate([top, bot], axis=0) * scale, vf, wvo, vp, vi, vh, va, 1)
     pair_sum(1)
     sc("ru_wait")
-    wait(ru.at[pl.ds(0, NZ - 1)], r_su)
+    wait(ru.at[pl.ds(0, NZ - 1 - len(hop))], r_su)
     sc("bwd_q")
     acc = su[0]
     for k in range(1, NZ):
-        acc = acc + ru[k]
+        if k not in hop:
+            acc = acc + ru[k]
     backward(jnp.transpose(acc) * scale, qf, wqo, up, ui, uh, ua, 0)
     pair_sum(0)
     plane_sum(1)
@@ -474,9 +493,10 @@
 
 def emit(fin, loss, gqi, gqo, gvi, gvo, loss_o):
     for t, (gi, go) in enumerate(((gqi, gqo), (gvi, gvo))):
-        gi[:, 0:128] = fin[t, 0:256]
-        gi[:, 128:256] = fin[t, 256:512]
-        go[...] = fin[t, 512:768]
+        full = fin[t].reshape(768, 128)
+        gi[:, 0:128] = full[0:256]
+        gi[:, 128:256] = full[256:512]
+        go[...] = full[512:768]
     loss_o[...] = loss[...]
 
 
@@ -491,7 +511,7 @@
         fin, loss = pl.pallas_call(
             functools.partial(kernel, NZ, NY, NX),
             name="two_tower",
-            out_shape=[sd((2, 2, NXY, CH, 128), f32), sd((1, 128), f32)],
+            out_shape=[pltpu.VMEM((2, 2, NXY, CH, 128), f32), pltpu.VMEM((1, 128), f32)],
             in_specs=[hbm] * 7,
             out_specs=[vm] * 2,
             scratch_shapes=[
@@ -501,13 +521,13 @@
                 V((NI, 128), f32), V((2, GR, 2 * R), f32), V((NI, NQ), f32), V((NI, NQ), bf16), V((2 * NXY, 8, NQ), f32),
                 V((NZ, 1, NQ + 256), f32), V((1, NQ), f32), V((1, NQ), f32),
                 *tower, *tower,
-                V((NZ, 128, 128), f32), V((NZ, 128, 128), f32),
+                V((NZ, 128, 128), f32), V((NZ, 128, 128), f32), V((NZ, 128, 128), f32),
                 V((NXY, 128, 128), f32), V((NXY, 128, 128), f32), V((NXY, 128, 128), f32),
                 V((NY, NX - 1, H, 128), f32), V((NX, NY - 1, H, 128), f32), V((NY, H, 128), f32), V((NX, H, 128), f32),
                 V((NY - 1, H, 128), f32), V((NX - 1, H, 128), f32), V((NY + NX - 2, H, 128), f32),
                 V((2, 768, 128), f32), V((2, 384, 128), f32), V((2, NXY, CH, 128), f32), V((2, NXY, CH, 128), f32),
                 V((2, NZ, CH, 128), f32), V((2, 1, 128), f32), V((NXY, 1, 128), f32),
-                S, S((NZ,)), S, S((2 * NXY,)), S, S, S, S, S((NXY,)), S, S, S((NY,)), S((NX,)), S, S, S, S,
+                S, S((NZ,)), S, S((2 * NXY,)), S, S, S, S, S((NXY,)), S, S, S((NY,)), S((NX,)), S, S, S, S, S((NZ,)),
                 S((2,)), S((2,)), S((2,)), S((2,)), S((2,)), S((2,)), S((2,)), S((2, NXY)), S((2,)), S((2, NXY)),
                 S, S, S, S, S,
             ],
@@ -519,7 +539,7 @@
             out_shape=[sd((256, 256), f32), sd((256, 128), f32), sd((256, 256), f32), sd((256, 128), f32), sd((1, 128), f32)],
             in_specs=[vm] * 2,
             out_specs=[vm] * 5,
-        )(fin.reshape(2, 768, 128), loss)
+        )(pltpu.with_memory_space_constraint(fin, pltpu.VMEM), pltpu.with_memory_space_constraint(loss, pltpu.VMEM))
         return out[0, 0:1], gqi, gqo, gvi, gvo
     return step
 

time: 65.3 us -> 63.2 us (0.968)
  Pallas kernels: 64.6 us -> 62.5 us
    pallas_call x1, Pallas kernels: 2.02 us -> 0.93 us  [step(): pl.pallas_call(emit, name='emit', out_shape=[sd((256, 256), f32), sd((256...]
    pallas_call x1, Pallas kernels: 62.5 us -> 61.5 us  [step(): pl.pallas_call(functools.partial(kernel, NZ, NY, NX), name='two_tower', o...]
where the time goes in v5:
time: 63.2 us; the launch traced here: 63.1 us
  Pallas kernels  62.5 us (99%)
  between operations  0.64 us (1%)
    pallas_call x1, Pallas kernels, step(): pl.pallas_call(functools.partial(kernel, NZ, NY, NX), name='two_tower', o...  61.5 us

profile of v5, /device:TPU:1, one launch (start us, length us, event | category | flops | bytes accessed | tf_op | source)
XLA Modules:
  0.0 63.1 jit_solution(2706171279495257755)
XLA Ops:
  0.6 61.5 %two_tower.1 = (f32[2,2,16,24,128]{4,3,2,1,0:T(8,128)S(1)}, f32[1,128]{1,0:T(1,128)S(1)}) custom-call(bf16[128,256]{1,0:T(8,128)(2,1)} %qf_h.1, bf16[128,256]{1,0:T(8,128)(2,1)} %vf_h.1, f32[1,128]{1,0:T(1,128)} %bitcast.3, bf16[256,256]{1,0:T(8,128)(2,1)} %wqi_h.1, bf16[256,128]{1,0:T(8,128)(2,1)} %wqo_h.1, bf16[256,256]{1,0:T(8,128)(2,1)} %wvi_h.1, ...), custom_call_target="tpu_custom_call" | custom-call | tf_op jit(solution)/shard_map/two_tower/pallas_call | solution.py:511
  62.2 0.9 %emit.1 = (f32[256,256]{1,0:T(8,128)}, f32[256,128]{1,0:T(8,128)}, f32[256,256]{1,0:T(8,128)}, f32[256,128]{1,0:T(8,128)}, f32[1,128]{1,0:T(1,128)}) custom-call(f32[2,2,16,24,128]{4,3,2,1,0:T(8,128)S(1)} %get-tuple-element.12.fin, f32[1,128]{1,0:T(1,128)S(1)} %get-tuple-element.13.loss), custom_call_target="tpu_custom_call" | custom-call | tf_op jit(solution)/shard_map/emit/pallas_call | solution.py:536

commit v6 on v5

--- a/solution.py
+++ b/solution.py
@@ -55,10 +55,10 @@
 
 def kernel(NZ, NY, NX, qf_h, vf_h, lq_h, wqi_h, wqo_h, wvi_h, wvo_h, fin, loss_o,
            qf, vf, lq, wqi, wqo, wvi, wvo, s_in,
-           u_all, v_all, vt, lq_all, mslot, wslot, cnt, bcol, sbuf, e_all, g_all, csum, stats, invl, invt,
+           u4, v_all, vt, lq_all, mslot, wslot, cnt, bcol, sbuf, e_all, g_all, csum, stats, invl, invt,
            up, ui, uh, ua, vp, vi, vh, va,
-           su, ru, hop_in, pv_out, pv_in, sv, rx, ry, tx, ty, r2x, r2y, t_cnt, gl, gpair, gx_s, gx_r, gz_r, loss_p, loss_x,
-           s_u, r_u, s_v, r_v, s_lq, s_st, r_st, s_pv, r_pv, s_p1, s_p2, r_x, r_y, r_2x, r_2y, s_su, r_su, r_hop,
+           su, ru, hop_in, sv, rv, v2, b2, w2, e2, g2, il4, gl, gpair, gx_s, gx_r, gz_r, loss_p, loss_x,
+           s_u, r_u, s_v, r_v, s_lq, s_st, r_st, s_sv, r_sv, s_u2, r_u2, s_il, r_il, s_su, r_su, r_hop,
            s_gp, r_gp, s_gx, r_gx, s_gz, r_gz, s_ag, r_ag, s_rl, r_rl, s_lp, r_lp, s_lx, r_lx, s_vr):
     sc = Scope()
     NXY = NY * NX
@@ -94,6 +94,9 @@
         xx = lax.rem(x + (b if sign > 0 else NX - b), NX)
         return yy * NX + xx
 
+    def ax(a, o):
+        return lax.rem(y + o * (1 - a), NY) * NX + lax.rem(x + o * a, NX)
+
     def slot(k, core):
         return (k // SL) * 2 * SL + core * SL + k % SL
 
@@ -112,6 +115,7 @@
     peers = [dev(zs(k, 1), j, c) for k in range(1, NZ)]
     peers += [dev(z, xs(k, 1), c) for k in range(1, NXY)]
     peers += [dev(z, j, oc)]
+    peers += [dev(z, ax(a, o), oc) for a in (0, 1) for o in range(1, NX)]
     for p in peers:
         pl.semaphore_signal(bar, inc=1, device_id=p, device_id_type=MESH)
     loads = [pltpu.make_async_copy(a, b, s_in.at[i]) for i, (a, b) in enumerate(
@@ -151,9 +155,9 @@
     send_item(0, slot(0, 1), s_vr, dev(z, j, oc))
     sc("tower_q")
     u_bf = tower(qf, wqi, wqo, up, ui, uh, ua, loads[4:7])
-    u_all[0:R, :] = u_bf
+    u4[0:R, :] = u_bf
     for k in range(1, NZ):
-        send(u_all.at[pl.ds(0, R), :], u_all.at[pl.ds(k * R, R), :], s_u, r_u.at[k], dev(zs(k, 1), j, c))
+        send(u4.at[pl.ds(0, R), :], u4.at[pl.ds(k * R, R), :], s_u, r_u.at[k], dev(zs(k, 1), j, c))
     pos = jnp.sum(u_bf.astype(f32) * v_bf.astype(f32), axis=0, keepdims=True) * (1.0 / TEMP) - lq[...]
     stats[z, :, pl.ds(NQ + 128, 128)] = pos
 
@@ -199,7 +203,11 @@
                     send_item(slot(k, 0), slot(k, 1), s_vr, dev(z, j, oc))
             for k in (2 * l, 2 * l + 1):
                 if k:
-                    wait(u_all.at[pl.ds(k * R, R), :], r_u.at[k])
+                    wait(u4.at[pl.ds(k * R, R), :], r_u.at[k])
+            if l >= LV - 2:
+                r0, nr = (0, (LV - 1) * QC) if l == LV - 2 else ((LV - 1) * QC, QC)
+                for b in ring(NX)[1:]:
+                    send(u4.at[pl.ds(r0, nr), :], u4.at[pl.ds(b * NQ + r0, nr), :], s_u2, r_u2.at[b], dev(z, ax(1 - c, b), c))
             fresh += groups(l, 0)
         if l:
             for k in range((l - 1) * SL, l * SL):
@@ -216,7 +224,7 @@
             tasks = [(g, l) for g in old] + tasks
         done += fresh
         for n, (g, l2) in enumerate(tasks):
-            sbuf[n % 2] = dot(v_all[grp(g), :], u_all[qcols(l2), :], NT)
+            sbuf[n % 2] = dot(v_all[grp(g), :], u4[qcols(l2), :], NT)
             if n:
                 expo(n - 1, *tasks[n - 1])
         expo(len(tasks) - 1, *tasks[-1])
@@ -235,6 +243,34 @@
     sc("transpose")
     for g in range(LV * NG):
         vt[:, grp(g)] = jnp.transpose(v_all[grp(g), :].astype(f32)).astype(bf16)
+    line = [(a, core) for a in ring(NX)[::-1] for core in (0, 1)]
+    at = []
+    for i, (a, core) in enumerate(line):
+        s0, s1 = (slot(xoff.index(o), core) for o in ((a, 0), (0, a)))
+        s = s0 + c * (s1 - s0)
+        at.append(s)
+        v2[i * R:(i + 1) * R, :] = v_all[pl.ds(s * R, R), :]
+        b2[i * R:(i + 1) * R, :] = bcol[pl.ds(s * R, R), :]
+        w2[i] = wslot[s]
+
+    def line_exp(bs):
+        sc(f"line{bs[0]}")
+        for b in bs:
+            wait(u4.at[pl.ds(b * NQ, NQ), :], r_u2.at[b])
+        tasks = [(g, b, l) for b in bs for g in range(len(line) // 2) for l in range(LV)]
+
+        def fin_exp(n, g, b, l):
+            bb = b2[grp(g), :]
+            e2[grp(g), (b - 1) * NQ + l * QC:(b - 1) * NQ + (l + 1) * QC] = jnp.exp2(
+                sbuf[n % 2] * (LOG2E / TEMP) - jnp.concatenate([bb, bb], axis=1))
+
+        for n, (g, b, l) in enumerate(tasks):
+            sbuf[n % 2] = dot(v2[grp(g), :], u4[b * NQ + l * QC:b * NQ + (l + 1) * QC, :], NT)
+            if n:
+                fin_exp(n - 1, *tasks[n - 1])
+        fin_exp(len(tasks) - 1, *tasks[-1])
+
+    near = ring(NX)[1:]
     sc("stats_wait")
     wait(stats.at[pl.ds(0, NZ - 1)], r_st)
     sc("stats_comp")
@@ -246,6 +282,9 @@
     invt[...] = jnp.concatenate([jnp.exp2((big - mx) * LOG2E)] * NZ, axis=1) / tot
     for k in range(NZ):
         invl[:, k * R:(k + 1) * R] = invt[:, pl.ds(pl.multiple_of(zs(k, -1) * R, R), R)]
+    il4[0] = invl[...]
+    for b in ring(NX)[1:]:
+        send(il4.at[0], il4.at[b], s_il, r_il.at[b], dev(z, ax(1 - c, b), c))
     lse = jnp.log2(tot) * LN2 + jnp.concatenate([mx] * NZ, axis=1)
     lrow = jnp.zeros((1, 128), f32)
     for k in range(NZ):
@@ -267,22 +306,6 @@
             out.append(p)
         return jnp.concatenate(out, axis=0)
 
-    pend = []
-    sv_of = {}
-    for k, (a, b) in enumerate(xoff):
-        sv_of[a, b] = k
-
-    def flush(keep):
-        while len(pend) > keep:
-            for k in pend.pop(0):
-                a, b = xoff[k]
-                wait(pv_in.at[k], r_pv.at[k])
-                sv[k] = sv[k] + pv_in[k]
-                if b:
-                    send(sv.at[k, pl.ds(0, H)], rx.at[a, b - 1], s_p1, r_x.at[a], dev(z, xs(sv_of[0, b], -1), c))
-                if a:
-                    send(sv.at[k, pl.ds(H, H)], ry.at[b, a - 1], s_p1, r_y.at[b], dev(z, xs(sv_of[a, 0], -1), c))
-
     normed = set()
 
     def ready(g, l):
@@ -290,30 +313,53 @@
             normed.add((g, l))
             norm(g, l, l + 1)
 
-    def dv_half(ls, core):
-        sc(f"dv{ls[0]}{core}")
-        ds = []
-        for l in ls:
-            gs = groups(l, core)
-            for g in gs:
-                for l2 in range(LV):
-                    ready(g, l2)
-            rows = [(gs[0] * GR, (gs[-1] + 1) * GR)] if len(ls) > 1 else [(g * GR, (g + 1) * GR) for g in gs]
-            ds += [(l, r0 - gs[0] * GR, dot(g_all[r0:r1, :], u_all[...])) for r0, r1 in rows]
-        keep = pv_out if core else sv
-        for l, r0, d in ds:
-            for i in range(d.shape[0] // R):
-                keep[l * SL + r0 // R + i] = d[i * R:(i + 1) * R, :]
-        for l in ls:
-            ks = list(range(l * SL, (l + 1) * SL))
-            if core:
-                for k in ks:
-                    send(pv_out.at[k], pv_in.at[k], s_pv, r_pv.at[k], dev(z, j, oc))
+    def line_norm(g, bs):
+        for i in (2 * g, 2 * g + 1):
+            for b in bs:
+                for l in range(LV):
+                    cols = slice(l * QC, (l + 1) * QC)
+                    f = il4[b, :, cols] * jnp.concatenate([w2[i], w2[i]], axis=1)
+                    if b:
+                        p = e2[i * R:(i + 1) * R, (b - 1) * NQ + l * QC:(b - 1) * NQ + (l + 1) * QC] * f
+                    else:
+                        p = e_all[pl.ds(pl.multiple_of(at[i] * R, R), R), cols] * f
+                    if line[i] == (0, 0) and b == 0 and l == 0:
+                        col = lax.broadcasted_iota(jnp.int32, p.shape, 1)
+                        p = jnp.where(lax.broadcasted_iota(jnp.int32, p.shape, 0) == col, p - 1.0, p)
+                    g2[i * R:(i + 1) * R, b * NQ + l * QC:b * NQ + (l + 1) * QC] = p.astype(bf16)
+
+    def line_dots(gs, k0, k1):
+        if len(gs) > 1:
+            ds = [dot(g2[grp(g), k0:k1], u4[k0:k1, :]) for g in gs]
+            ds = [d[i * R:(i + 1) * R] for d in ds for i in range(2)]
+        else:
+            ds = [dot(g2[i * R:(i + 1) * R, k0:k1], u4[k0:k1, :]) for i in (2 * gs[0], 2 * gs[0] + 1)]
+        return [i for g in gs for i in (2 * g, 2 * g + 1)], ds
+
+    def line_own():
+        sc("ldv_own")
+        gs = list(range(len(line) // 2))
+        for g in gs:
+            line_norm(g, [0])
+        for i, d in zip(*line_dots(gs, 0, NQ)):
+            sv[i] = d
+
+    def line_dv(gs):
+        sc(f"ldv{gs[0]}")
+        for g in gs:
+            line_norm(g, range(1, NX))
+        idx, ds = line_dots(gs, NQ, NX * NQ)
+        for i, d in zip(idx, ds):
+            a, core = line[i]
+            d = sv[i] + d
+            if a or core:
+                sv[i] = d
             else:
-                pend.append(ks)
-        if not core:
-            sc(f"flush{ls[0]}")
-            flush(0)
+                rv[c * NX] = d
+        for i in idx:
+            a, core = line[i]
+            if a or core:
+                send(sv.at[i], rv.at[c * NX + a], s_sv, r_sv, dev(z, ax(c, NX - a), oc if core else c))
 
     def du_levels(ls):
         sc(f"du{ls[0]}")
@@ -349,33 +395,26 @@
             send(su.at[k], ru.at[k], s_su, r_su, dev(zs(k, -1), j, c))
 
     if LV == 4:
-        dv_half([1, 2], 1)
         du_levels([1, 2])
-        dv_half([1, 2], 0)
-        dv_half([3, 0], 1)
+        line_own()
+        line_exp(near[:2])
+        line_exp(near[2:])
+        sc("il_wait")
+        for b in near:
+            wait(il4.at[b], r_il.at[b])
+        line_dv([0])
         du_levels([3, 0])
-        dv_half([3, 0], 0)
+        line_dv([1, 2])
+        line_dv([3])
         send_late()
     else:
-        dv_half([0, 1], 1)
         du_levels([1, 0])
-        dv_half([0, 1], 0)
-
-    def leg2(o, own, r1, sem1, t1, r2, sem2, far):
-        wait(r1.at[o], sem1.at[o])
-        acc = own
-        for i in range(r1.shape[1]):
-            acc = acc + r1[o, i]
-        t1[o] = acc
-        if o:
-            send(t1.at[o], r2.at[o - 1], s_p2, sem2, far)
-
-    sc("leg2")
-    for o in ring(max(NY, NX))[::-1]:
-        if o < NY:
-            leg2(o, sv[sv_of[o, 0], 0:H], rx, r_x, tx, r2x, r_2x, dev(z, xs(sv_of[o, 0], -1), c))
-        if o < NX:
-            leg2(o, sv[sv_of[0, o], H:R], ry, r_y, ty, r2y, r_2y, dev(z, xs(sv_of[0, o], -1), c))
+        line_exp(near)
+        line_own()
+        for b in near:
+            wait(il4.at[b], r_il.at[b])
+        line_dv([0])
+        line_dv([1])
 
     sc("loss")
     wait(loss_p.at[oc], r_lp)
@@ -434,15 +473,12 @@
 
     scale = 1.0 / (TEMP * B)
     sc("rv_wait")
-    wait(r2x, r_2x)
-    wait(r2y, r_2y)
+    wait(rv.at[pl.ds(0, 2 * NX - 1)], r_sv)
     sc("bwd_v")
-    top, bot = tx[0], ty[0]
-    for i in range(NY - 1):
-        top = top + r2x[i]
-    for i in range(NX - 1):
-        bot = bot + r2y[i]
-    backward(jnp.concatenate([top, bot], axis=0) * scale, vf, wvo, vp, vi, vh, va, 1)
+    acc = rv[0]
+    for i in range(1, 2 * NX):
+        acc = acc + rv[i]
+    backward(acc * scale, vf, wvo, vp, vi, vh, va, 1)
     pair_sum(1)
     sc("ru_wait")
     wait(ru.at[pl.ds(0, NZ - 1 - len(hop))], r_su)
@@ -472,14 +508,14 @@
 
     sc("sendwait")
     wait(lq_all.at[pl.ds(0, 2 * NXY - 1)], s_lq)
-    wait(u_all.at[pl.ds(0, (NZ - 1) * R), :], s_u)
+    wait(u4.at[pl.ds(0, (NZ - 1) * R), :], s_u)
     wait(v_all.at[pl.ds(0, (NXY - 1) * R), :], s_v)
     wait(v_all.at[pl.ds(0, NXY * R), :], s_vr)
     wait(stats.at[pl.ds(0, NZ - 1)], s_st)
     wait(loss_p.at[0], s_lp)
-    wait(pv_out, s_pv)
-    wait(sv.at[pl.ds(0, (NY * (NX - 1) + NX * (NY - 1)) // 2)], s_p1)
-    wait(t_cnt, s_p2)
+    wait(sv.at[pl.ds(0, 2 * NX - 1)], s_sv)
+    wait(u4.at[pl.ds(NQ, (NX - 1) * NQ), :], s_u2)
+    wait(il4.at[pl.ds(1, NX - 1)], s_il)
     wait(su.at[pl.ds(0, NZ - 1)], s_su)
     wait(loss_x.at[pl.ds(0, NXY - 1)], s_lx)
     for t in range(2):
@@ -517,17 +553,17 @@
             scratch_shapes=[
                 V((R, 256), bf16), V((R, 256), bf16), V((1, 128), f32),
                 V((256, 256), bf16), V((256, 128), bf16), V((256, 256), bf16), V((256, 128), bf16), S((7,)),
-                V((NQ, 128), bf16), V((NI, 128), bf16), V((128, NI), bf16), V((2 * NXY, 1, 128), f32), V((2 * NXY, 1, 128), f32), V((2 * NXY, 1, 128), f32), V((65, 1, 128), f32),
+                V((NX * NQ, 128), bf16), V((NI, 128), bf16), V((128, NI), bf16), V((2 * NXY, 1, 128), f32), V((2 * NXY, 1, 128), f32), V((2 * NXY, 1, 128), f32), V((65, 1, 128), f32),
                 V((NI, 128), f32), V((2, GR, 2 * R), f32), V((NI, NQ), f32), V((NI, NQ), bf16), V((2 * NXY, 8, NQ), f32),
                 V((NZ, 1, NQ + 256), f32), V((1, NQ), f32), V((1, NQ), f32),
                 *tower, *tower,
                 V((NZ, 128, 128), f32), V((NZ, 128, 128), f32), V((NZ, 128, 128), f32),
-                V((NXY, 128, 128), f32), V((NXY, 128, 128), f32), V((NXY, 128, 128), f32),
-                V((NY, NX - 1, H, 128), f32), V((NX, NY - 1, H, 128), f32), V((NY, H, 128), f32), V((NX, H, 128), f32),
-                V((NY - 1, H, 128), f32), V((NX - 1, H, 128), f32), V((NY + NX - 2, H, 128), f32),
+                V((2 * NX, 128, 128), f32), V((2 * NX, 128, 128), f32),
+                V((2 * NX * R, 128), bf16), V((2 * NX * R, 128), f32), V((2 * NX, 1, 128), f32),
+                V((2 * NX * R, (NX - 1) * NQ), f32), V((2 * NX * R, NX * NQ), bf16), V((NX, 1, NQ), f32),
                 V((2, 768, 128), f32), V((2, 384, 128), f32), V((2, NXY, CH, 128), f32), V((2, NXY, CH, 128), f32),
                 V((2, NZ, CH, 128), f32), V((2, 1, 128), f32), V((NXY, 1, 128), f32),
-                S, S((NZ,)), S, S((2 * NXY,)), S, S, S, S, S((NXY,)), S, S, S((NY,)), S((NX,)), S, S, S, S, S((NZ,)),
+                S, S((NZ,)), S, S((2 * NXY,)), S, S, S, S, S, S, S((NX,)), S, S((NX,)), S, S, S((NZ,)),
                 S((2,)), S((2,)), S((2,)), S((2,)), S((2,)), S((2,)), S((2,)), S((2, NXY)), S((2,)), S((2, NXY)),
                 S, S, S, S, S,
             ],

time: 63.2 us -> 61.2 us (0.968)
  Pallas kernels: 62.5 us -> 60.5 us
    pallas_call x1, Pallas kernels: 61.5 us -> 59.5 us  [step(): pl.pallas_call(functools.partial(kernel, NZ, NY, NX), name='two_tower', o...]
where the time goes in v6:
time: 61.2 us; the launch traced here: 61.1 us
  Pallas kernels  60.5 us (99%)
  between operations  0.64 us (1%)
    pallas_call x1, Pallas kernels, step(): pl.pallas_call(functools.partial(kernel, NZ, NY, NX), name='two_tower', o...  59.5 us

profile of v6, /device:TPU:1, one launch (start us, length us, event | category | flops | bytes accessed | tf_op | source)
XLA Modules:
  0.0 61.1 jit_solution(11508948056817820575)
XLA Ops:
  0.6 59.5 %two_tower.1 = (f32[2,2,16,24,128]{4,3,2,1,0:T(8,128)S(1)}, f32[1,128]{1,0:T(1,128)S(1)}) custom-call(bf16[128,256]{1,0:T(8,128)(2,1)} %qf_h.1, bf16[128,256]{1,0:T(8,128)(2,1)} %vf_h.1, f32[1,128]{1,0:T(1,128)} %bitcast.3, bf16[256,256]{1,0:T(8,128)(2,1)} %wqi_h.1, bf16[256,128]{1,0:T(8,128)(2,1)} %wqo_h.1, bf16[256,256]{1,0:T(8,128)(2,1)} %wvi_h.1, ...), custom_call_target="tpu_custom_call" | custom-call | tf_op jit(solution)/shard_map/two_tower/pallas_call | solution.py:547
  60.2 0.9 %emit.1 = (f32[256,256]{1,0:T(8,128)}, f32[256,128]{1,0:T(8,128)}, f32[256,256]{1,0:T(8,128)}, f32[256,128]{1,0:T(8,128)}, f32[1,128]{1,0:T(1,128)}) custom-call(f32[2,2,16,24,128]{4,3,2,1,0:T(8,128)S(1)} %get-tuple-element.12.fin, f32[1,128]{1,0:T(1,128)S(1)} %get-tuple-element.13.loss), custom_call_target="tpu_custom_call" | custom-call | tf_op jit(solution)/shard_map/emit/pallas_call | solution.py:572

commit v7 on v6

--- a/solution.py
+++ b/solution.py
@@ -18,7 +18,7 @@
 NN = (((1,), (0,)), ((), ()))
 R = 128
 GR = 256
-H = R // 2
+ROWS = (256, 512), (384, 384)
 
 
 class Scope:
@@ -65,7 +65,6 @@
     NQ = NZ * R
     NI = 2 * NXY * R
     B = NZ * NI
-    CH = 384 // NXY
     LV = NZ // 2
     SL = NXY // LV
     QC = 2 * R
@@ -387,9 +386,10 @@
             hop[zoff.index(o)] = (o - via) % NZ
             late[zoff.index(via)] = zoff.index(o)
 
-    def send_late():
+    def send_late(ks):
         sc("late")
-        for k, k2 in late.items():
+        for k in ks:
+            k2 = late[k]
             wait(hop_in.at[k2], r_hop.at[k2])
             su[k] = su[k] + hop_in[k2]
             send(su.at[k], ru.at[k], s_su, r_su, dev(zs(k, -1), j, c))
@@ -403,10 +403,11 @@
         for b in near:
             wait(il4.at[b], r_il.at[b])
         line_dv([0])
+        line_dv([1, 2])
         du_levels([3, 0])
-        line_dv([1, 2])
+        send_late([k for k in late if k // 2 == 2])
         line_dv([3])
-        send_late()
+        send_late([k for k in late if k // 2 != 2])
     else:
         du_levels([1, 0])
         line_exp(near)
@@ -421,6 +422,18 @@
     loss_x[j] = loss_p[0] + loss_p[1]
     for k in range(1, NXY):
         send(loss_x.at[j], loss_x.at[j], s_lx, r_lx, dev(z, xs(k, 1), c))
+
+    def per_core(f):
+        for core in (0, 1):
+            @pl.when(c == core)
+            def _():
+                f(core)
+
+    def chunk(t, core):
+        return ROWS[t][core] // NXY
+
+    def rows_of(t, core, k):
+        return pl.ds(pl.multiple_of(k * chunk(t, core), 8), chunk(t, core))
 
     def backward(du, xr, wo, unit, inv, hid, act, t):
         u, r = unit[...], inv[...]
@@ -432,44 +445,66 @@
         gl[t, 0:256, :] = gi[:, 0:128]
         gl[t, 256:512, :] = gi[:, 128:256]
         gl[t, 512:768, :] = go
-        send(gl.at[t, pl.ds(pl.multiple_of(oc * 384, 8), 384), :], gpair.at[t], s_gp.at[t], r_gp.at[t], dev(z, j, oc))
+
+        @per_core
+        def _(core):
+            o = 1 - core
+            send(gl.at[t, pl.ds(o * ROWS[t][0], ROWS[t][o]), :], gpair.at[t, pl.ds(0, ROWS[t][o]), :], s_gp.at[t], r_gp.at[t], dev(z, j, oc))
 
     def pair_sum(t):
         sc(f"gp_wait{t}")
-        wait(gpair.at[t], r_gp.at[t])
-        gx_s[t] = (gl[t, pl.ds(pl.multiple_of(c * 384, 8), 384), :] + gpair[t]).reshape(NXY, CH, 128)
-        for k in xfar:
-            to = xs(k, 1)
-            send(gx_s.at[t, to], gx_r.at[t, j], s_gx.at[t], r_gx.at[t], dev(z, to, c))
-        gx_r[t, j] = gx_s[t, j]
+
+        @per_core
+        def _(core):
+            wait(gpair.at[t, pl.ds(0, ROWS[t][core]), :], r_gp.at[t])
+            gx_s[t, 0:ROWS[t][core], :] = gl[t, core * ROWS[t][0]:core * ROWS[t][0] + ROWS[t][core], :] + gpair[t, 0:ROWS[t][core], :]
+            for k in xfar:
+                to = xs(k, 1)
+                send(gx_s.at[t, rows_of(t, core, to), :], gx_r.at[t, rows_of(t, core, j), :], s_gx.at[t], r_gx.at[t], dev(z, to, c))
+            gx_r[t, rows_of(t, core, j), :] = gx_s[t, rows_of(t, core, j), :]
 
     def plane_sum(t):
         sc(f"gx_wait{t}")
-        wait(gx_r.at[t, pl.ds(0, NXY - 1)], r_gx.at[t])
-        acc = gx_r[t, 0]
-        for k in range(1, NXY):
-            acc = acc + gx_r[t, k]
-        gz_r[t, z] = acc
-        for k in zfar:
-            send(gz_r.at[t, z], gz_r.at[t, z], s_gz.at[t], r_gz.at[t], dev(zs(k, 1), j, c))
+
+        @per_core
+        def _(core):
+            n = chunk(t, core)
+            wait(gx_r.at[t, pl.ds(0, (NXY - 1) * n), :], r_gx.at[t])
+            acc = gx_r[t, 0:n, :]
+            for k in range(1, NXY):
+                acc = acc + gx_r[t, k * n:(k + 1) * n, :]
+            gz_r[t, rows_of(t, core, z), :] = acc
+            for k in zfar:
+                send(gz_r.at[t, rows_of(t, core, z), :], gz_r.at[t, rows_of(t, core, z), :], s_gz.at[t], r_gz.at[t], dev(zs(k, 1), j, c))
+
+    def part(t, core, jj):
+        return fin.at[t, pl.ds(pl.multiple_of(core * ROWS[t][0] + jj * chunk(t, core), 8), chunk(t, core)), :]
 
     def ring_sum(t):
         sc(f"gz_wait{t}")
-        wait(gz_r.at[t, pl.ds(0, NZ - 1)], r_gz.at[t])
-        acc = gz_r[t, 0]
-        for k in range(1, NZ):
-            acc = acc + gz_r[t, k]
-        fin[t, c, j] = acc
-        for k in xfar:
-            send(fin.at[t, c, j], fin.at[t, c, j], s_ag.at[t], r_ag.at[t, k], dev(z, xs(k, 1), c))
-        send(fin.at[t, c, j], fin.at[t, c, j], s_rl.at[t], r_rl.at[t, 0], dev(z, j, oc))
+
+        @per_core
+        def _(core):
+            n = chunk(t, core)
+            wait(gz_r.at[t, pl.ds(0, (NZ - 1) * n), :], r_gz.at[t])
+            acc = gz_r[t, 0:n, :]
+            for k in range(1, NZ):
+                acc = acc + gz_r[t, k * n:(k + 1) * n, :]
+            mine = part(t, core, j)
+            mine[...] = acc
+            for k in xfar:
+                send(mine, mine, s_ag.at[t], r_ag.at[t, k], dev(z, xs(k, 1), c))
+            send(mine, mine, s_rl.at[t], r_rl.at[t, 0], dev(z, j, oc))
 
     def relay(t):
         sc(f"ag_wait{t}")
-        for k in xfar:
-            ref = fin.at[t, c, xs(k, -1)]
-            wait(ref, r_ag.at[t, k])
-            send(ref, ref, s_rl.at[t], r_rl.at[t, k], dev(z, j, oc))
+
+        @per_core
+        def _(core):
+            for k in xfar:
+                ref = part(t, core, xs(k, -1))
+                wait(ref, r_ag.at[t, k])
+                send(ref, ref, s_rl.at[t], r_rl.at[t, k], dev(z, j, oc))
 
     scale = 1.0 / (TEMP * B)
     sc("rv_wait")
@@ -489,22 +524,25 @@
             acc = acc + ru[k]
     backward(jnp.transpose(acc) * scale, qf, wqo, up, ui, uh, ua, 0)
     pair_sum(0)
+    sc("loss2")
+    wait(loss_x.at[pl.ds(0, NXY - 1)], r_lx)
+    ls = loss_x[0]
+    for k in range(1, NXY):
+        ls = ls + loss_x[k]
+    loss_o[...] = jnp.broadcast_to(jnp.sum(ls, axis=-1, keepdims=True) * (1.0 / B), (1, 128))
     plane_sum(1)
     plane_sum(0)
     ring_sum(1)
     ring_sum(0)
     relay(1)
     relay(0)
-    sc("loss2")
-    wait(loss_x.at[pl.ds(0, NXY - 1)], r_lx)
-    ls = loss_x[0]
-    for k in range(1, NXY):
-        ls = ls + loss_x[k]
-    loss_o[...] = jnp.broadcast_to(jnp.sum(ls, axis=-1, keepdims=True) * (1.0 / B), (1, 128))
     sc("rl_wait")
-    for t in range(2):
-        for k in range(NXY):
-            wait(fin.at[t, oc, xs(k, -1)], r_rl.at[t, k])
+
+    @per_core
+    def _(core):
+        for t in range(2):
+            for k in range(NXY):
+                wait(part(t, 1 - core, xs(k, -1)), r_rl.at[t, k])
 
     sc("sendwait")
     wait(lq_all.at[pl.ds(0, 2 * NXY - 1)], s_lq)
@@ -518,28 +556,35 @@
     wait(il4.at[pl.ds(1, NX - 1)], s_il)
     wait(su.at[pl.ds(0, NZ - 1)], s_su)
     wait(loss_x.at[pl.ds(0, NXY - 1)], s_lx)
-    for t in range(2):
-        wait(gpair.at[t], s_gp.at[t])
-        wait(gx_s.at[t, pl.ds(0, NXY - 1)], s_gx.at[t])
-        wait(gz_r.at[t, pl.ds(0, NZ - 1)], s_gz.at[t])
-        wait(gx_s.at[t, pl.ds(0, NXY - 1)], s_ag.at[t])
-        wait(gx_s.at[t], s_rl.at[t])
+
+    @per_core
+    def _(core):
+        for t in range(2):
+            n = chunk(t, core)
+            wait(gpair.at[t, pl.ds(0, ROWS[t][1 - core]), :], s_gp.at[t])
+            wait(gx_s.at[t, pl.ds(0, (NXY - 1) * n), :], s_gx.at[t])
+            wait(gz_r.at[t, pl.ds(0, (NZ - 1) * n), :], s_gz.at[t])
+            wait(gx_s.at[t, pl.ds(0, (NXY - 1) * n), :], s_ag.at[t])
+            wait(gx_s.at[t, pl.ds(0, NXY * n), :], s_rl.at[t])
+
     sc(None)
 
 
-def emit(fin, loss, gqi, gqo, gvi, gvo, loss_o):
+def emit(fin, loss, gqi, gqo, gvi, gvo, loss_o, sem):
+    copies = [(loss, loss_o)]
     for t, (gi, go) in enumerate(((gqi, gqo), (gvi, gvo))):
-        full = fin[t].reshape(768, 128)
-        gi[:, 0:128] = full[0:256]
-        gi[:, 128:256] = full[256:512]
-        go[...] = full[512:768]
-    loss_o[...] = loss[...]
+        copies += [(fin.at[t, 0:256, :], gi.at[:, 0:128]), (fin.at[t, 256:512, :], gi.at[:, 128:256]), (fin.at[t, 512:768, :], go)]
+    copies = [pltpu.make_async_copy(a, b, sem.at[i]) for i, (a, b) in enumerate(copies)]
+    for cp in copies:
+        cp.start()
+    for cp in copies:
+        cp.wait()
 
 
 def build(NZ, NY, NX):
     def step(query_feat, item_feat, log_q, w_query_in, w_query_out, w_item_in, w_item_out):
         NXY = NY * NX
-        NQ, NI, CH = NZ * R, 2 * NXY * R, 384 // NXY
+        NQ, NI = NZ * R, 2 * NXY * R
         V, S = pltpu.VMEM, pltpu.SemaphoreType.DMA
         vm, hbm = pl.BlockSpec(memory_space=pltpu.VMEM), pl.BlockSpec(memory_space=pl.ANY)
         sd = jax.ShapeDtypeStruct
@@ -547,7 +592,7 @@
         fin, loss = pl.pallas_call(
             functools.partial(kernel, NZ, NY, NX),
             name="two_tower",
-            out_shape=[pltpu.VMEM((2, 2, NXY, CH, 128), f32), pltpu.VMEM((1, 128), f32)],
+            out_shape=[pltpu.VMEM((2, 768, 128), f32), pltpu.VMEM((1, 128), f32)],
             in_specs=[hbm] * 7,
             out_specs=[vm] * 2,
             scratch_shapes=[
@@ -561,8 +606,8 @@
                 V((2 * NX, 128, 128), f32), V((2 * NX, 128, 128), f32),
                 V((2 * NX * R, 128), bf16), V((2 * NX * R, 128), f32), V((2 * NX, 1, 128), f32),
                 V((2 * NX * R, (NX - 1) * NQ), f32), V((2 * NX * R, NX * NQ), bf16), V((NX, 1, NQ), f32),
-                V((2, 768, 128), f32), V((2, 384, 128), f32), V((2, NXY, CH, 128), f32), V((2, NXY, CH, 128), f32),
-                V((2, NZ, CH, 128), f32), V((2, 1, 128), f32), V((NXY, 1, 128), f32),
+                V((2, 768, 128), f32), V((2, max(map(max, ROWS)), 128), f32), V((2, max(map(max, ROWS)), 128), f32), V((2, max(map(max, ROWS)), 128), f32),
+                V((2, NZ * max(map(max, ROWS)) // NXY, 128), f32), V((2, 1, 128), f32), V((NXY, 1, 128), f32),
                 S, S((NZ,)), S, S((2 * NXY,)), S, S, S, S, S, S, S((NX,)), S, S((NX,)), S, S, S((NZ,)),
                 S((2,)), S((2,)), S((2,)), S((2,)), S((2,)), S((2,)), S((2,)), S((2, NXY)), S((2,)), S((2, NXY)),
                 S, S, S, S, S,
@@ -574,7 +619,8 @@
             name="emit",
             out_shape=[sd((256, 256), f32), sd((256, 128), f32), sd((256, 256), f32), sd((256, 128), f32), sd((1, 128), f32)],
             in_specs=[vm] * 2,
-            out_specs=[vm] * 5,
+            out_specs=[hbm] * 5,
+            scratch_shapes=[S((7,))],
         )(pltpu.with_memory_space_constraint(fin, pltpu.VMEM), pltpu.with_memory_space_constraint(loss, pltpu.VMEM))
         return out[0, 0:1], gqi, gqo, gvi, gvo
     return step

time: 61.2 us -> 60.7 us (level)
  no operation moved by 1% of the time
where the time goes in v7:
time: 60.7 us; the launch traced here: 60.6 us
  Pallas kernels  59.9 us (99%)
  between operations  0.64 us (1%)
    pallas_call x1, Pallas kernels, step(): pl.pallas_call(functools.partial(kernel, NZ, NY, NX), name='two_tower', o...  59 us

profile of v7, /device:TPU:1, one launch (start us, length us, event | category | flops | bytes accessed | tf_op | source)
XLA Modules:
  0.0 60.6 jit_solution(10600955427836882600)
XLA Ops:
  0.6 59.0 %two_tower.1 = (f32[2,768,128]{2,1,0:T(8,128)S(1)}, f32[1,128]{1,0:T(1,128)S(1)}) custom-call(bf16[128,256]{1,0:T(8,128)(2,1)} %qf_h.1, bf16[128,256]{1,0:T(8,128)(2,1)} %vf_h.1, f32[1,128]{1,0:T(1,128)} %bitcast.3, bf16[256,256]{1,0:T(8,128)(2,1)} %wqi_h.1, bf16[256,128]{1,0:T(8,128)(2,1)} %wqo_h.1, bf16[256,256]{1,0:T(8,128)(2,1)} %wvi_h.1, ...), custom_call_target="tpu_custom_call" | custom-call | tf_op jit(solution)/shard_map/two_tower/pallas_call | solution.py:592
  59.6 0.9 %emit.1 = (f32[256,256]{1,0:T(8,128)}, f32[256,128]{1,0:T(8,128)}, f32[256,256]{1,0:T(8,128)}, f32[256,128]{1,0:T(8,128)}, f32[1,128]{1,0:T(1,128)}) custom-call(f32[2,768,128]{2,1,0:T(8,128)S(1)} %get-tuple-element.12.fin, f32[1,128]{1,0:T(1,128)S(1)} %get-tuple-element.13.loss), custom_call_target="tpu_custom_call" | custom-call | tf_op jit(solution)/shard_map/emit/pallas_call | solution.py:617

commit v8 on v7

--- a/solution.py
+++ b/solution.py
@@ -17,7 +17,8 @@
 TN = (((0,), (0,)), ((), ()))
 NN = (((1,), (0,)), ((), ()))
 R = 128
-GR = 256
+W = 256
+GR = 2 * R
 ROWS = (256, 512), (384, 384)
 
 
@@ -132,7 +133,7 @@
         r = lax.rsqrt(jnp.sum(e * e, axis=-1, keepdims=True) + EPS)
         u = e * r
         unit[...] = u
-        inv[...] = jnp.broadcast_to(r, (R, 128))
+        inv[...] = jnp.broadcast_to(r, (R, R))
         hid[...] = h
         act[...] = a
         return u.astype(bf16)
@@ -158,28 +159,22 @@
     for k in range(1, NZ):
         send(u4.at[pl.ds(0, R), :], u4.at[pl.ds(k * R, R), :], s_u, r_u.at[k], dev(zs(k, 1), j, c))
     pos = jnp.sum(u_bf.astype(f32) * v_bf.astype(f32), axis=0, keepdims=True) * (1.0 / TEMP) - lq[...]
-    stats[z, :, pl.ds(NQ + 128, 128)] = pos
+    stats[z, :, pl.ds(NQ + R, R)] = pos
 
     def grp(g):
         return slice(g * GR, (g + 1) * GR)
 
-    def dyn(g):
-        return pl.ds(pl.multiple_of(g * GR, GR), GR)
-
     def qcols(l):
         return slice(l * QC, (l + 1) * QC)
 
-    def loop(lo, n, f):
-        lax.fori_loop(0, n, lambda i, u: (f(lo + i), u)[1], 0)
-
     def bias(s0):
-        q = lq_all[s0:s0 + SL].reshape(SL, 128)
+        q = lq_all[s0:s0 + SL].reshape(SL, R)
         big = jnp.max(-q, axis=1, keepdims=True)
         b = (big + q) * LOG2E
         bt = jnp.transpose(jnp.concatenate([b] * (8 // SL), axis=0))
         for i in range(SL):
-            mslot[s0 + i] = jnp.broadcast_to(big[i:i + 1, :], (1, 128))
-            bcol[(s0 + i) * R:(s0 + i + 1) * R, :] = jnp.broadcast_to(bt[:, i:i + 1], (R, 128))
+            mslot[s0 + i] = jnp.broadcast_to(big[i:i + 1, :], (1, R))
+            bcol[(s0 + i) * R:(s0 + i + 1) * R, :] = jnp.broadcast_to(bt[:, i:i + 1], (R, R))
 
     def expo(n, g, l):
         rows, cols = grp(g), qcols(l)
@@ -230,7 +225,7 @@
 
     sc("stats_send")
     big = jnp.max(mslot[...], axis=0)
-    stats[z, :, pl.ds(NQ, 128)] = big
+    stats[z, :, pl.ds(NQ, R)] = big
     wslot[...] = jnp.exp2((mslot[...] - big) * LOG2E)
     for k in range(NZ):
         acc = csum[0, :, k * R:(k + 1) * R] * wslot[0]
@@ -273,7 +268,7 @@
     sc("stats_wait")
     wait(stats.at[pl.ds(0, NZ - 1)], r_st)
     sc("stats_comp")
-    ms = [stats[k, :, NQ:NQ + 128] for k in range(NZ)]
+    ms = [stats[k, :, NQ:NQ + R] for k in range(NZ)]
     mx = functools.reduce(jnp.maximum, ms)
     tot = jnp.zeros((1, NQ), f32)
     for k in range(NZ):
@@ -285,9 +280,9 @@
     for b in ring(NX)[1:]:
         send(il4.at[0], il4.at[b], s_il, r_il.at[b], dev(z, ax(1 - c, b), c))
     lse = jnp.log2(tot) * LN2 + jnp.concatenate([mx] * NZ, axis=1)
-    lrow = jnp.zeros((1, 128), f32)
+    lrow = jnp.zeros((1, R), f32)
     for k in range(NZ):
-        lrow = lrow + (lse[:, k * R:(k + 1) * R] - stats[k, :, NQ + 128:NQ + 256])
+        lrow = lrow + (lse[:, k * R:(k + 1) * R] - stats[k, :, NQ + R:NQ + W])
     loss_p[c] = lrow
     send(loss_p.at[c], loss_p.at[c], s_lp, r_lp, dev(z, j, oc))
 
@@ -394,28 +389,19 @@
             su[k] = su[k] + hop_in[k2]
             send(su.at[k], ru.at[k], s_su, r_su, dev(zs(k, -1), j, c))
 
-    if LV == 4:
-        du_levels([1, 2])
-        line_own()
-        line_exp(near[:2])
-        line_exp(near[2:])
-        sc("il_wait")
-        for b in near:
-            wait(il4.at[b], r_il.at[b])
-        line_dv([0])
-        line_dv([1, 2])
-        du_levels([3, 0])
-        send_late([k for k in late if k // 2 == 2])
-        line_dv([3])
-        send_late([k for k in late if k // 2 != 2])
-    else:
-        du_levels([1, 0])
-        line_exp(near)
-        line_own()
-        for b in near:
-            wait(il4.at[b], r_il.at[b])
-        line_dv([0])
-        line_dv([1])
+    du_levels([1, 2])
+    line_own()
+    line_exp(near[:2])
+    line_exp(near[2:])
+    sc("il_wait")
+    for b in near:
+        wait(il4.at[b], r_il.at[b])
+    line_dv([0])
+    line_dv([1, 2])
+    du_levels([3, 0])
+    send_late([k for k in late if k // 2 == 2])
+    line_dv([3])
+    send_late([k for k in late if k // 2 != 2])
 
     sc("loss")
     wait(loss_p.at[oc], r_lp)
@@ -442,8 +428,8 @@
         dh = dot(de, wo[...], NT)
         da = jnp.where(act[...] > 0, dh, 0.0).astype(bf16)
         gi = dot(xr[...], da, TN)
-        gl[t, 0:256, :] = gi[:, 0:128]
-        gl[t, 256:512, :] = gi[:, 128:256]
+        gl[t, 0:W, :] = gi[:, 0:R]
+        gl[t, W:512, :] = gi[:, R:W]
         gl[t, 512:768, :] = go
 
         @per_core
@@ -529,7 +515,7 @@
     ls = loss_x[0]
     for k in range(1, NXY):
         ls = ls + loss_x[k]
-    loss_o[...] = jnp.broadcast_to(jnp.sum(ls, axis=-1, keepdims=True) * (1.0 / B), (1, 128))
+    loss_o[...] = jnp.broadcast_to(jnp.sum(ls, axis=-1, keepdims=True) * (1.0 / B), (1, R))
     plane_sum(1)
     plane_sum(0)
     ring_sum(1)
@@ -573,7 +559,7 @@
 def emit(fin, loss, gqi, gqo, gvi, gvo, loss_o, sem):
     copies = [(loss, loss_o)]
     for t, (gi, go) in enumerate(((gqi, gqo), (gvi, gvo))):
-        copies += [(fin.at[t, 0:256, :], gi.at[:, 0:128]), (fin.at[t, 256:512, :], gi.at[:, 128:256]), (fin.at[t, 512:768, :], go)]
+        copies += [(fin.at[t, 0:W, :], gi.at[:, 0:R]), (fin.at[t, W:512, :], gi.at[:, R:W]), (fin.at[t, 512:768, :], go)]
     copies = [pltpu.make_async_copy(a, b, sem.at[i]) for i, (a, b) in enumerate(copies)]
     for cp in copies:
         cp.start()
@@ -588,36 +574,36 @@
         V, S = pltpu.VMEM, pltpu.SemaphoreType.DMA
         vm, hbm = pl.BlockSpec(memory_space=pltpu.VMEM), pl.BlockSpec(memory_space=pl.ANY)
         sd = jax.ShapeDtypeStruct
-        tower = [V((R, 128), f32), V((R, 128), f32), V((R, 256), bf16), V((R, 256), f32)]
+        tower = [V((R, R), f32), V((R, R), f32), V((R, W), bf16), V((R, W), f32)]
         fin, loss = pl.pallas_call(
             functools.partial(kernel, NZ, NY, NX),
             name="two_tower",
-            out_shape=[pltpu.VMEM((2, 768, 128), f32), pltpu.VMEM((1, 128), f32)],
+            out_shape=[pltpu.VMEM((2, 768, R), f32), pltpu.VMEM((1, R), f32)],
             in_specs=[hbm] * 7,
             out_specs=[vm] * 2,
             scratch_shapes=[
-                V((R, 256), bf16), V((R, 256), bf16), V((1, 128), f32),
-                V((256, 256), bf16), V((256, 128), bf16), V((256, 256), bf16), V((256, 128), bf16), S((7,)),
-                V((NX * NQ, 128), bf16), V((NI, 128), bf16), V((128, NI), bf16), V((2 * NXY, 1, 128), f32), V((2 * NXY, 1, 128), f32), V((2 * NXY, 1, 128), f32), V((65, 1, 128), f32),
-                V((NI, 128), f32), V((2, GR, 2 * R), f32), V((NI, NQ), f32), V((NI, NQ), bf16), V((2 * NXY, 8, NQ), f32),
-                V((NZ, 1, NQ + 256), f32), V((1, NQ), f32), V((1, NQ), f32),
+                V((R, W), bf16), V((R, W), bf16), V((1, R), f32),
+                V((W, W), bf16), V((W, R), bf16), V((W, W), bf16), V((W, R), bf16), S((7,)),
+                V((NX * NQ, R), bf16), V((NI, R), bf16), V((R, NI), bf16), V((2 * NXY, 1, R), f32), V((2 * NXY, 1, R), f32), V((2 * NXY, 1, R), f32), V((65, 1, R), f32),
+                V((NI, R), f32), V((2, GR, 2 * R), f32), V((NI, NQ), f32), V((NI, NQ), bf16), V((2 * NXY, 8, NQ), f32),
+                V((NZ, 1, NQ + W), f32), V((1, NQ), f32), V((1, NQ), f32),
                 *tower, *tower,
-                V((NZ, 128, 128), f32), V((NZ, 128, 128), f32), V((NZ, 128, 128), f32),
-                V((2 * NX, 128, 128), f32), V((2 * NX, 128, 128), f32),
-                V((2 * NX * R, 128), bf16), V((2 * NX * R, 128), f32), V((2 * NX, 1, 128), f32),
+                V((NZ, R, R), f32), V((NZ, R, R), f32), V((NZ, R, R), f32),
+                V((2 * NX, R, R), f32), V((2 * NX, R, R), f32),
+                V((2 * NX * R, R), bf16), V((2 * NX * R, R), f32), V((2 * NX, 1, R), f32),
                 V((2 * NX * R, (NX - 1) * NQ), f32), V((2 * NX * R, NX * NQ), bf16), V((NX, 1, NQ), f32),
-                V((2, 768, 128), f32), V((2, max(map(max, ROWS)), 128), f32), V((2, max(map(max, ROWS)), 128), f32), V((2, max(map(max, ROWS)), 128), f32),
-                V((2, NZ * max(map(max, ROWS)) // NXY, 128), f32), V((2, 1, 128), f32), V((NXY, 1, 128), f32),
+                V((2, 768, R), f32), V((2, max(map(max, ROWS)), R), f32), V((2, max(map(max, ROWS)), R), f32), V((2, max(map(max, ROWS)), R), f32),
+                V((2, NZ * max(map(max, ROWS)) // NXY, R), f32), V((2, 1, R), f32), V((NXY, 1, R), f32),
                 S, S((NZ,)), S, S((2 * NXY,)), S, S, S, S, S, S, S((NX,)), S, S((NX,)), S, S, S((NZ,)),
                 S((2,)), S((2,)), S((2,)), S((2,)), S((2,)), S((2,)), S((2,)), S((2, NXY)), S((2,)), S((2, NXY)),
                 S, S, S, S, S,
             ],
             compiler_params=pltpu.CompilerParams(collective_id=0, has_side_effects=True, vmem_limit_bytes=60 * 2**20),
-        )(query_feat, item_feat, log_q.reshape(1, 128), w_query_in, w_query_out, w_item_in, w_item_out)
+        )(query_feat, item_feat, log_q.reshape(1, R), w_query_in, w_query_out, w_item_in, w_item_out)
         gqi, gqo, gvi, gvo, out = pl.pallas_call(
             emit,
             name="emit",
-            out_shape=[sd((256, 256), f32), sd((256, 128), f32), sd((256, 256), f32), sd((256, 128), f32), sd((1, 128), f32)],
+            out_shape=[sd((W, W), f32), sd((W, R), f32), sd((W, W), f32), sd((W, R), f32), sd((1, R), f32)],
             in_specs=[vm] * 2,
             out_specs=[hbm] * 5,
             scratch_shapes=[S((7,))],
@@ -627,8 +613,6 @@
 
 
 def solution(mesh):
-    n = mesh.shape["dp"]
-    dims = (8, 4, 4) if n == 256 else (4, 2, 2)
-    return jax.shard_map(build(*dims), mesh=mesh,
+    return jax.shard_map(build(8, 4, 4), mesh=mesh,
                          in_specs=(P("dp", None), P("dp", None), P("dp"), P(), P(), P(), P()),
                          out_specs=(P(), P(), P(), P(), P()), check_vma=False)

time: 60.7 us -> 60.7 us (level)
  no operation moved by 1% of the time
where the time goes in v8:
time: 60.7 us; the launch traced here: 60.6 us
  Pallas kernels  59.9 us (99%)
  between operations  0.64 us (1%)
    pallas_call x1, Pallas kernels, step(): pl.pallas_call(functools.partial(kernel, NZ, NY, NX), name='two_tower', o...  59 us

profile of v8, /device:TPU:1, one launch (start us, length us, event | category | flops | bytes accessed | tf_op | source)
XLA Modules:
  0.0 60.6 jit_solution(10600955427836882600)
XLA Ops:
  0.6 59.0 %two_tower.1 = (f32[2,768,128]{2,1,0:T(8,128)S(1)}, f32[1,128]{1,0:T(1,128)S(1)}) custom-call(bf16[128,256]{1,0:T(8,128)(2,1)} %qf_h.1, bf16[128,256]{1,0:T(8,128)(2,1)} %vf_h.1, f32[1,128]{1,0:T(1,128)} %bitcast.3, bf16[256,256]{1,0:T(8,128)(2,1)} %wqi_h.1, bf16[256,128]{1,0:T(8,128)(2,1)} %wqo_h.1, bf16[256,256]{1,0:T(8,128)(2,1)} %wvi_h.1, ...), custom_call_target="tpu_custom_call" | custom-call | tf_op jit(solution)/shard_map/two_tower/pallas_call | solution.py:578
  59.6 0.9 %emit.1 = (f32[256,256]{1,0:T(8,128)}, f32[256,128]{1,0:T(8,128)}, f32[256,256]{1,0:T(8,128)}, f32[256,128]{1,0:T(8,128)}, f32[1,128]{1,0:T(1,128)}) custom-call(f32[2,768,128]{2,1,0:T(8,128)S(1)} %get-tuple-element.12.fin, f32[1,128]{1,0:T(1,128)S(1)} %get-tuple-element.13.loss), custom_call_target="tpu_custom_call" | custom-call | tf_op jit(solution)/shard_map/emit/pallas_call | solution.py:603

commit v9 on v8

--- a/solution.py
+++ b/solution.py
@@ -60,7 +60,7 @@
            up, ui, uh, ua, vp, vi, vh, va,
            su, ru, hop_in, sv, rv, v2, b2, w2, e2, g2, il4, gl, gpair, gx_s, gx_r, gz_r, loss_p, loss_x,
            s_u, r_u, s_v, r_v, s_lq, s_st, r_st, s_sv, r_sv, s_u2, r_u2, s_il, r_il, s_su, r_su, r_hop,
-           s_gp, r_gp, s_gx, r_gx, s_gz, r_gz, s_ag, r_ag, s_rl, r_rl, s_lp, r_lp, s_lx, r_lx, s_vr):
+           s_gp, r_gp, s_gx, r_gx, s_gz, r_gz, s_ag, r_ag, s_rl, r_rl, s_lp, r_lp, s_lx, r_lx, s_vr, order):
     sc = Scope()
     NXY = NY * NX
     NQ = NZ * R
@@ -106,6 +106,10 @@
 
     def wait(ref, sem):
         pltpu.make_async_copy(ref, ref, sem).wait()
+
+    def fence():
+        pl.semaphore_signal(order, inc=1)
+        pl.semaphore_wait(order, 1)
 
     def vrows(s):
         return v_all.at[pl.ds(s * R, R), :]
@@ -234,6 +238,7 @@
         stats[z, :, pl.ds(pl.multiple_of(zs(k, -1) * R, R), R)] = jnp.sum(acc, axis=0, keepdims=True)
     for k in zfar:
         send(stats.at[z], stats.at[z], s_st, r_st, dev(zs(k, 1), j, c))
+    fence()
     sc("transpose")
     for g in range(LV * NG):
         vt[:, grp(g)] = jnp.transpose(v_all[grp(g), :].astype(f32)).astype(bf16)
@@ -279,6 +284,7 @@
     il4[0] = invl[...]
     for b in ring(NX)[1:]:
         send(il4.at[0], il4.at[b], s_il, r_il.at[b], dev(z, ax(1 - c, b), c))
+    fence()
     lse = jnp.log2(tot) * LN2 + jnp.concatenate([mx] * NZ, axis=1)
     lrow = jnp.zeros((1, R), f32)
     for k in range(NZ):
@@ -390,17 +396,25 @@
             send(su.at[k], ru.at[k], s_su, r_su, dev(zs(k, -1), j, c))
 
     du_levels([1, 2])
+    fence()
     line_own()
+    fence()
     line_exp(near[:2])
+    fence()
     line_exp(near[2:])
+    fence()
     sc("il_wait")
     for b in near:
         wait(il4.at[b], r_il.at[b])
     line_dv([0])
+    fence()
     line_dv([1, 2])
+    fence()
     du_levels([3, 0])
+    fence()
     send_late([k for k in late if k // 2 == 2])
     line_dv([3])
+    fence()
     send_late([k for k in late if k // 2 != 2])
 
     sc("loss")
@@ -596,7 +610,7 @@
                 V((2, NZ * max(map(max, ROWS)) // NXY, R), f32), V((2, 1, R), f32), V((NXY, 1, R), f32),
                 S, S((NZ,)), S, S((2 * NXY,)), S, S, S, S, S, S, S((NX,)), S, S((NX,)), S, S, S((NZ,)),
                 S((2,)), S((2,)), S((2,)), S((2,)), S((2,)), S((2,)), S((2,)), S((2, NXY)), S((2,)), S((2, NXY)),
-                S, S, S, S, S,
+                S, S, S, S, S, pltpu.SemaphoreType.REGULAR,
             ],
             compiler_params=pltpu.CompilerParams(collective_id=0, has_side_effects=True, vmem_limit_bytes=60 * 2**20),
         )(query_feat, item_feat, log_q.reshape(1, R), w_query_in, w_query_out, w_item_in, w_item_out)

time: 60.7 us -> 60.2 us (level)
  no operation moved by 1% of the time
where the time goes in v9:
time: 60.2 us; the launch traced here: 60.1 us
  Pallas kernels  59.5 us (99%)
  between operations  0.64 us (1%)
    pallas_call x1, Pallas kernels, step(): pl.pallas_call(functools.partial(kernel, NZ, NY, NX), name='two_tower', o...  58.6 us

profile of v9, /device:TPU:1, one launch (start us, length us, event | category | flops | bytes accessed | tf_op | source)
XLA Modules:
  0.0 60.1 jit_solution(9035237965475295353)
XLA Ops:
  0.6 58.6 %two_tower.1 = (f32[2,768,128]{2,1,0:T(8,128)S(1)}, f32[1,128]{1,0:T(1,128)S(1)}) custom-call(bf16[128,256]{1,0:T(8,128)(2,1)} %qf_h.1, bf16[128,256]{1,0:T(8,128)(2,1)} %vf_h.1, f32[1,128]{1,0:T(1,128)} %bitcast.3, bf16[256,256]{1,0:T(8,128)(2,1)} %wqi_h.1, bf16[256,128]{1,0:T(8,128)(2,1)} %wqo_h.1, bf16[256,256]{1,0:T(8,128)(2,1)} %wvi_h.1, ...), custom_call_target="tpu_custom_call" | custom-call | tf_op jit(solution)/shard_map/two_tower/pallas_call | solution.py:592
  59.2 0.9 %emit.1 = (f32[256,256]{1,0:T(8,128)}, f32[256,128]{1,0:T(8,128)}, f32[256,256]{1,0:T(8,128)}, f32[256,128]{1,0:T(8,128)}, f32[1,128]{1,0:T(1,128)}) custom-call(f32[2,768,128]{2,1,0:T(8,128)S(1)} %get-tuple-element.12.fin, f32[1,128]{1,0:T(1,128)S(1)} %get-tuple-element.13.loss), custom_call_target="tpu_custom_call" | custom-call | tf_op jit(solution)/shard_map/emit/pallas_call | solution.py:617
